TPU v7x, 32 devices: a whole 2x2x4 slice. The times are simulated.
32 devices in a mesh: dp: 16 (over z, x, core), mp: 2 (over y).
Axes of the slice: x: 2, y: 2, z: 4, core: 2. Of those that a mesh axis runs over, the one named last changes fastest.
Arguments:
- ranges: bfloat16 [512, 2652], P(('dp', 'mp')), may hold values from 0.0099487305 to 1
- board: int32 [512, 5], P(('dp', 'mp')), may hold values from 0 to 51, as said below
- targets: bfloat16 [512, 2652], P(('dp', 'mp')), may hold values from -6 to 6
- w_in: bfloat16 [1536, 2704], P(('mp', 'dp')), may hold values from -0.34570312 to 0.34570312
- w_out: bfloat16 [1536, 2652], P(('mp', 'dp')), may hold values from -0.3046875 to 0.3046875
Outputs:
- predicted: bfloat16 [512, 2652], P(('dp', 'mp'))
- update_in: float32 [1536, 2704], P(('mp', 'dp'))
- update_out: float32 [1536, 2652], P(('mp', 'dp'))
- loss: float32 [], replicated
Inputs may be any that keep to these rules, and one draw needn't show every extreme that they name: `board`: each row holds 5 different cards.
All inputs are finite; a program needn't handle non-finite values.
Results may differ from a plain program's by a relative error of at most 0.014.
Values may be sent and summed in bfloat16 or wider, within the bound.
No kernel may reach another device: no remote copies, remote signals or barrier semaphores. Data moves between devices by JAX's collectives and lax.ppermute only.
A program may use at most 64 MiB of HBM per device.

v0:
```python
import functools

import jax
import jax.numpy as jnp
from jax import lax
from jax.experimental import pallas as pl
from jax.experimental.pallas import tpu as pltpu
from jax.sharding import PartitionSpec as P


CARDS = 52


def huber_terms(error_value):
    magnitude = jnp.abs(error_value)
    return jnp.where(magnitude <= 1.0, 0.5 * error_value * error_value, magnitude - 0.5)


def build_features(ranges, board):
    card_ids = jnp.arange(CARDS, dtype=jnp.int32)
    onehot_board = jnp.sum(
        (board[:, :, None] == card_ids[None, None, :]).astype(jnp.float32), axis=1
    ).astype(jnp.bfloat16)
    return jnp.concatenate([ranges, onehot_board], axis=1)


def right_product(left_side, right_block):
    return lax.dot_general(
        left_side, right_block, (((1,), (1,)), ((), ())), preferred_element_type=jnp.float32
    )


def left_product(left_side, right_side):
    return lax.dot_general(
        left_side, right_side, (((0,), (0,)), ((), ())), preferred_element_type=jnp.float32
    )


def gather_weights_body(ranges, board, targets, w_in, w_out):
    mp_count = lax.axis_size("mp")
    dp_count = lax.axis_size("dp")
    stored_rows = ranges.shape[0]
    value_width = w_out.shape[1]
    all_ranges = lax.all_gather(ranges, "mp", axis=0, tiled=True)
    all_board = lax.all_gather(board, "mp", axis=0, tiled=True)
    features = build_features(all_ranges, all_board)
    local_in = lax.all_gather(w_in, "dp", axis=0, tiled=True)
    preact = right_product(features, local_in)
    hidden = jax.nn.gelu(preact).astype(jnp.bfloat16)
    local_out = lax.all_gather(w_out, "dp", axis=0, tiled=True)
    partial_value = jnp.dot(hidden, local_out, preferred_element_type=jnp.float32)
    stacked = partial_value.astype(jnp.bfloat16).reshape(mp_count, stored_rows, value_width)
    received = lax.all_to_all(stacked, "mp", split_axis=0, concat_axis=0, tiled=True)
    summed = jnp.sum(received.astype(jnp.float32), axis=0)
    error_value = summed - targets.astype(jnp.float32)
    own_grad = jnp.clip(error_value, -1.0, 1.0).astype(jnp.bfloat16)
    out_grad = lax.all_gather(own_grad, "mp", axis=0, tiled=True)
    predicted = summed.astype(jnp.bfloat16)
    loss_part = jnp.sum(huber_terms(error_value))
    grad_out = lax.psum_scatter(
        left_product(hidden, out_grad), "dp", scatter_dimension=0, tiled=True
    )
    hidden_grad = right_product(out_grad, local_out)
    _, gelu_back = jax.vjp(jax.nn.gelu, preact)
    preact_grad = gelu_back(hidden_grad)[0].astype(jnp.bfloat16)
    grad_in = lax.psum_scatter(
        left_product(preact_grad, features), "dp", scatter_dimension=0, tiled=True
    )
    square_part = jnp.sum(grad_in * grad_in) + jnp.sum(grad_out * grad_out)
    loss_total, square_total = lax.psum((loss_part, square_part), ("dp", "mp"))
    device_count = mp_count * dp_count
    count_params = w_in.shape[0] * device_count * (w_in.shape[1] + value_width)
    scale = lax.rsqrt(square_total / count_params + 1e-06)
    loss = loss_total / (stored_rows * device_count * value_width)
    return (predicted, grad_in * scale, grad_out * scale, loss)


def exchange(block, axes, step):
    count = lax.axis_size(axes)
    return lax.ppermute(block, axes, [(index, index ^ step) for index in range(count)])


def split_rows(whole, count):
    size = whole.shape[0] // count
    return [whole[index * size : (index + 1) * size] for index in range(count)]


def gather_states(rows):
    near = [rows]
    for step in range(1, lax.axis_size("z")):
        near.append(exchange(rows, ("z",), step))
    far = []
    for block in near:
        far.append(exchange(block, ("c",), 1))
    return jnp.concatenate(near + far, axis=0)


def gather_units(w_in, w_out):
    in_y = exchange(w_in, ("y",), 1)
    out_x = exchange(w_out, ("x",), 1)
    in_x = exchange(w_in, ("x",), 1)
    out_y = exchange(w_out, ("y",), 1)
    in_xy = exchange(in_y, ("x",), 1)
    out_xy = exchange(out_x, ("y",), 1)

    def ordered(own, along_x, along_y, diagonal):
        own, along_x, along_y, diagonal = (split_rows(rows, 2) for rows in (own, along_x, along_y, diagonal))
        first = [own[0], along_y[0], along_x[0], diagonal[0]]
        return jnp.concatenate(first + [own[1], along_x[1], along_y[1], diagonal[1]], axis=0)

    return ordered(w_in, in_x, in_y, in_xy), ordered(w_out, out_x, out_y, out_xy)


def plane_sum(left, right):
    upper_pair, upper_far, lower_pair, lower_far = (block.T for block in split_rows(left.T, 4))
    upper_got = exchange(left_product(upper_far, right).astype(jnp.bfloat16), ("x",), 1)
    lower_got = exchange(left_product(lower_far, right).astype(jnp.bfloat16), ("y",), 1)
    upper_own, upper_next = split_rows(left_product(upper_pair, right), 2)
    lower_own, lower_next = split_rows(left_product(lower_pair, right), 2)
    upper_got_own, upper_got_next = split_rows(upper_got, 2)
    lower_got_own, lower_got_next = split_rows(lower_got, 2)
    upper_next = (upper_next + upper_got_next.astype(jnp.float32)).astype(jnp.bfloat16)
    lower_next = (lower_next + lower_got_next.astype(jnp.float32)).astype(jnp.bfloat16)
    upper_last = exchange(upper_next, ("y",), 1)
    lower_last = exchange(lower_next, ("x",), 1)
    upper_near = upper_own + upper_got_own.astype(jnp.float32)
    lower_near = lower_own + lower_got_own.astype(jnp.float32)
    return upper_near, upper_last, lower_near, lower_last


def closing_kernel(*refs):
    loss_part, grad_in, grad_out, copies = refs[8:]
    square = 0.0
    for parts, grad in ((refs[:4], grad_in), (refs[4:8], grad_out)):
        half = grad.shape[0] // 2
        for index in range(2):
            near, last = parts[2 * index : 2 * index + 2]
            total = near[...] + last[...].astype(jnp.float32)
            grad[index * half : (index + 1) * half] = total
            square = square + jnp.sum(total * total)
    lane = lax.broadcasted_iota(jnp.int32, copies.shape, 1)
    copies[...] = jnp.where(lane == 0, square, jnp.where(lane == 1, loss_part[0], 0.0))


def scaling_kernel(param_count, value_count, copies, grad_in, grad_out, update_in, update_out, loss):
    lane = lax.broadcasted_iota(jnp.int32, copies.shape, 1)
    values = copies[...]
    square = jnp.sum(jnp.where(lane == 0, values, 0.0), keepdims=True)
    scale = lax.rsqrt(square / param_count + 1e-06)
    update_in[...] = grad_in[...] * scale
    update_out[...] = grad_out[...] * scale
    loss[0] = jnp.sum(jnp.where(lane == 1, values, 0.0)) / value_count


def in_vmem(array):
    return pltpu.with_memory_space_constraint(array, pltpu.VMEM)


def torus_body(ranges, board, targets, w_in, w_out):
    z_count = lax.axis_size("z")
    device_count = z_count * lax.axis_size(("x", "y", "c"))
    stored_rows = ranges.shape[0]
    value_width = w_out.shape[1]
    units_in, units_out = gather_units(w_in, w_out)
    features = gather_states(build_features(ranges, board))
    preact = right_product(features, units_in)
    hidden = jax.nn.gelu(preact).astype(jnp.bfloat16)
    own_hidden, other_hidden = split_rows(hidden, 2)
    other_value = jnp.dot(other_hidden, units_out, preferred_element_type=jnp.float32).astype(jnp.bfloat16)
    other_got = exchange(other_value, ("c",), 1)
    own_value = jnp.dot(own_hidden, units_out, preferred_element_type=jnp.float32)
    chip_value = split_rows(own_value + other_got.astype(jnp.float32), z_count)
    summed = chip_value[0]
    received = [exchange(chip_value[k].astype(jnp.bfloat16), ("z",), k) for k in range(1, z_count)]
    for part in received:
        summed = summed + part.astype(jnp.float32)
    error_value = summed - targets.astype(jnp.float32)
    out_grad = gather_states(jnp.clip(error_value, -1.0, 1.0).astype(jnp.bfloat16))
    predicted = summed.astype(jnp.bfloat16)
    loss_part = jnp.sum(huber_terms(error_value))
    parts_out = plane_sum(hidden, out_grad)
    hidden_grad = right_product(out_grad, units_out)
    _, gelu_back = jax.vjp(jax.nn.gelu, preact)
    preact_grad = lax.optimization_barrier(gelu_back(hidden_grad)[0].astype(jnp.bfloat16))
    parts_in = plane_sum(preact_grad, features)
    vector = pl.BlockSpec(memory_space=pltpu.VMEM)
    scalar = pl.BlockSpec(memory_space=pltpu.SMEM)
    grad_in, grad_out, copies = pl.pallas_call(
        closing_kernel,
        out_shape=(
            pltpu.VMEM(w_in.shape, jnp.float32),
            pltpu.VMEM(w_out.shape, jnp.float32),
            pltpu.VMEM((device_count, 128), jnp.float32),
        ),
        in_specs=[vector] * 8 + [scalar],
        out_specs=(vector, vector, vector),
    )(*(in_vmem(part) for part in parts_in + parts_out), loss_part.reshape(1))
    copies = lax.all_to_all(copies, ("z", "x", "c", "y"), split_axis=0, concat_axis=0, tiled=True)
    param_count = w_in.shape[0] * device_count * (w_in.shape[1] + value_width)
    value_count = stored_rows * device_count * value_width
    update_in, update_out, loss = pl.pallas_call(
        functools.partial(scaling_kernel, param_count, value_count),
        out_shape=(
            jax.ShapeDtypeStruct(w_in.shape, jnp.float32),
            jax.ShapeDtypeStruct(w_out.shape, jnp.float32),
            jax.ShapeDtypeStruct((1,), jnp.float32),
        ),
        in_specs=[vector, vector, vector],
        out_specs=(vector, vector, scalar),
    )(in_vmem(copies), in_vmem(grad_in), in_vmem(grad_out))
    return (predicted, update_in, update_out, loss.reshape(()))


def layer_body(*arrays):
    return torus_body(*arrays)


def torus_mesh(mesh):
    devices = mesh.devices
    chips = [tuple(device.coords) for device in devices.flat]
    z_count = len({chip[2] for chip in chips})
    x_count = len({chip[0] for chip in chips})
    core_count = devices.size // len(set(chips))
    shape = (z_count, x_count, core_count, devices.shape[1])
    return jax.sharding.Mesh(devices.reshape(shape), ("z", "x", "c", "y"))


def solution(mesh):
    def step(ranges, board, targets, w_in, w_out):
        batch_fits = ranges.shape[0] <= w_in.shape[0] // mesh.shape["mp"]
        if batch_fits:
            used_mesh, body = torus_mesh(mesh), layer_body
            rows, units = P(("z", "x", "c", "y"), None), P(("y", "z", "x", "c"), None)
        else:
            used_mesh, body = mesh, gather_weights_body
            rows, units = P(("dp", "mp"), None), P(("mp", "dp"), None)
        mapped = jax.shard_map(
            body,
            mesh=used_mesh,
            in_specs=(rows, rows, rows, units, units),
            out_specs=(rows, units, units, P()),
            check_vma=False,
        )
        return mapped(ranges, board, targets, w_in, w_out)

    return step
```

profile of v0, /device:TPU:0, one launch (start us, length us, event | category | flops | bytes accessed | tf_op | source)
XLA Modules:
  0.0 100.7 jit_solution(7428790453760316291)
XLA Ops:
  0.6 0.8 convert_reduce_fusion
  1.5 1.0 pad_maximum_fusion
  2.4 3.1 %collective-permute-start = (bf16[16,2704]{1,0:T(8,128)(2,1)S(1)}, bf16[16,2704]{1,0:T(8,128)(2,1)S(1)}, u32[]{:S(2)}, u32[]{:S(2)}) collective-permute-start(bf16[16,2704]{1,0:T(8,128)(2,1)S(1)} %get-tuple-element.31), channel_id=1, source_target_pairs={{0,8},{8,0},{16,24},{24,16},{1,9},{9,1},{17,25},{25,17},{2,10},{10... | collective-permute-start | bytes 259592 | tf_op jit(solution)/shard_map/ppermute | solution.py:80
  5.5 2.6 %collective-permute-start.1 = (bf16[16,2704]{1,0:T(8,128)(2,1)S(1)}, bf16[16,2704]{1,0:T(8,128)(2,1)S(1)}, u32[]{:S(2)}, u32[]{:S(2)}) collective-permute-start(bf16[16,2704]{1,0:T(8,128)(2,1)S(1)} %get-tuple-element.31), channel_id=1, source_target_pairs={{0,16},{8,24},{16,0},{24,8},{1,17},{9,25},{17,1},{25,9},{2,18},{10... | collective-permute-start | bytes 259592 | tf_op jit(solution)/shard_map/ppermute | solution.py:80
  8.1 1.7 %collective-permute-start.7 = (bf16[48,2704]{1,0:T(8,128)(2,1)}, bf16[48,2704]{1,0:T(8,128)(2,1)S(1)}, u32[]{:S(2)}, u32[]{:S(2)}) collective-permute-start(bf16[48,2704]{1,0:T(8,128)(2,1)} %param.8), channel_id=1, source_target_pairs={{0,1},{1,0},{2,3},{3,2},{4,5},{5,4},{6,7},{7,6},{8,9},{9,8},{10,11... | collective-permute-start | bytes 778760 | tf_op jit(solution)/shard_map/ppermute | solution.py:80
  9.8 0.9 slice_dynamic-update-slice_fusion.7
  10.8 0.9 slice_dynamic-update-slice_fusion.15
  11.7 1.6 %collective-permute-start.8 = (bf16[48,2704]{1,0:T(8,128)(2,1)}, bf16[48,2704]{1,0:T(8,128)(2,1)S(1)}, u32[]{:S(2)}, u32[]{:S(2)}) collective-permute-start(bf16[48,2704]{1,0:T(8,128)(2,1)} %param.8), channel_id=1, source_target_pairs={{0,4},{4,0},{1,5},{5,1},{2,6},{6,2},{3,7},{7,3},{8,12},{12,8},{9,1... | collective-permute-start | bytes 778760 | tf_op jit(solution)/shard_map/ppermute | solution.py:80
  13.3 2.0 %collective-permute-done.1 = bf16[16,2704]{1,0:T(8,128)(2,1)S(1)} collective-permute-done((bf16[16,2704]{1,0:T(8,128)(2,1)S(1)}, bf16[16,2704]{1,0:T(8,128)(2,1)S(1)}, u32[]{:S(2)}, u32[]{:S(2)}) %collective-permute-start.1) | collective-permute-done | bytes 86560 | tf_op jit(solution)/shard_map/ppermute | solution.py:80
  15.3 1.5 %collective-permute-start.11 = (bf16[48,2652]{1,0:T(8,128)(2,1)}, bf16[48,2652]{1,0:T(8,128)(2,1)S(1)}, u32[]{:S(2)}, u32[]{:S(2)}) collective-permute-start(bf16[48,2652]{1,0:T(8,128)(2,1)} %param.9), channel_id=1, source_target_pairs={{0,4},{4,0},{1,5},{5,1},{2,6},{6,2},{3,7},{7,3},{8,12},{12,8},{9,1... | collective-permute-start | bytes 763784 | tf_op jit(solution)/shard_map/ppermute | solution.py:80
  16.8 1.6 %collective-permute-start.10 = (bf16[48,2652]{1,0:T(8,128)(2,1)S(1)}, bf16[48,2652]{1,0:T(8,128)(2,1)S(1)}, u32[]{:S(2)}, u32[]{:S(2)}) collective-permute-start(bf16[48,2652]{1,0:T(8,128)(2,1)S(1)} %copy-done.2), channel_id=1, source_target_pairs={{0,1},{1,0},{2,3},{3,2},{4,5},{5,4},{6,7},{7,6},{8,9},{9,8},{10,11... | collective-permute-start | bytes 763784 | tf_op jit(solution)/shard_map/ppermute | solution.py:80
  18.5 1.3 %collective-permute-done.4 = bf16[16,2704]{1,0:T(8,128)(2,1)S(1)} collective-permute-done((bf16[16,2704]{1,0:T(8,128)(2,1)S(1)}, bf16[16,2704]{1,0:T(8,128)(2,1)S(1)}, u32[]{:S(2)}, u32[]{:S(2)}) %collective-permute-start.4) | collective-permute-done | bytes 86560 | tf_op jit(solution)/shard_map/ppermute | solution.py:80
  19.8 0.2 collective-permute-start.5
  19.9 1.1 %collective-permute-done.5 = bf16[16,2704]{1,0:T(8,128)(2,1)S(1)} collective-permute-done((bf16[16,2704]{1,0:T(8,128)(2,1)S(1)}, bf16[16,2704]{1,0:T(8,128)(2,1)S(1)}, u32[]{:S(2)}, u32[]{:S(2)}) %collective-permute-start.5) | collective-permute-done | bytes 86560 | tf_op jit(solution)/shard_map/ppermute | solution.py:80
  21.2 1.1 %collective-permute-done.6 = bf16[16,2704]{1,0:T(8,128)(2,1)S(1)} collective-permute-done((bf16[16,2704]{1,0:T(8,128)(2,1)S(1)}, bf16[16,2704]{1,0:T(8,128)(2,1)S(1)}, u32[]{:S(2)}, u32[]{:S(2)}) %collective-permute-start.6) | collective-permute-done | bytes 86560 | tf_op jit(solution)/shard_map/ppermute | solution.py:80
  22.3 3.8 %collective-permute-done.11 = bf16[48,2652]{1,0:T(8,128)(2,1)S(1)} collective-permute-done((bf16[48,2652]{1,0:T(8,128)(2,1)}, bf16[48,2652]{1,0:T(8,128)(2,1)S(1)}, u32[]{:S(2)}, u32[]{:S(2)}) %collective-permute-start.11) | collective-permute-done | bytes 254624 | tf_op jit(solution)/shard_map/ppermute | solution.py:80
  26.1 0.3 collective-permute-start.12
  26.5 1.8 %collective-permute-start.9 = (bf16[48,2704]{1,0:T(8,128)(2,1)S(1)}, bf16[48,2704]{1,0:T(8,128)(2,1)S(1)}, u32[]{:S(2)}, u32[]{:S(2)}) collective-permute-start(bf16[48,2704]{1,0:T(8,128)(2,1)S(1)} %collective-permute-done.7), channel_id=1, source_target_pairs={{0,4},{4,0},{1,5},{5,1},{2,6},{6,2},{3,7},{7,3},{8,12},{12,8},{9,1... | collective-permute-start | bytes 778760 | tf_op jit(solution)/shard_map/ppermute | solution.py:80
  28.3 5.3 %collective-permute-done.12 = bf16[48,2652]{1,0:T(8,128)(2,1)S(1)} collective-permute-done((bf16[48,2652]{1,0:T(8,128)(2,1)S(1)}, bf16[48,2652]{1,0:T(8,128)(2,1)S(1)}, u32[]{:S(2)}, u32[]{:S(2)}) %collective-permute-start.12) | collective-permute-done | bytes 254624 | tf_op jit(solution)/shard_map/ppermute | solution.py:80
  33.7 0.3 collective-permute-done.9
  34.1 0.5 multiply_convert_fusion
  34.6 0.4 convolution_convert_fusion
  35.1 1.6 %collective-permute-done.13 = bf16[64,2652]{1,0:T(8,128)(2,1)S(1)} collective-permute-done((bf16[64,2652]{1,0:T(8,128)(2,1)S(1)}, bf16[64,2652]{1,0:T(8,128)(2,1)S(1)}, u32[]{:S(2)}, u32[]{:S(2)}) %collective-permute-start.13) | collective-permute-done | bytes 339488 | tf_op jit(solution)/shard_map/ppermute | solution.py:80
  36.7 0.3 fusion.39
  37.1 1.0 collective-permute-start.14
  38.1 3.5 %collective-permute-start.15 = (bf16[16,2652]{1,0:T(8,128)(2,1)S(1)}, bf16[16,2652]{1,0:T(8,128)(2,1)S(1)}, u32[]{:S(2)}, u32[]{:S(2)}) collective-permute-start(bf16[16,2652]{1,0:T(8,128)(2,1)S(1)} %get-tuple-element.30), channel_id=1, source_target_pairs={{0,16},{8,24},{16,0},{24,8},{1,17},{9,25},{17,1},{25,9},{2,18},{10... | collective-permute-start | bytes 254600 | tf_op jit(solution)/shard_map/ppermute | solution.py:80
  41.6 0.2 collective-permute-done.14
  41.7 6.8 %collective-permute-done.15 = bf16[16,2652]{1,0:T(8,128)(2,1)S(1)} collective-permute-done((bf16[16,2652]{1,0:T(8,128)(2,1)S(1)}, bf16[16,2652]{1,0:T(8,128)(2,1)S(1)}, u32[]{:S(2)}, u32[]{:S(2)}) %collective-permute-start.15) | collective-permute-done | bytes 84896 | tf_op jit(solution)/shard_map/ppermute | solution.py:80
  48.5 0.7 fusion.5
  49.2 1.8 %collective-permute-start.17 = (bf16[16,2652]{1,0:T(8,128)(2,1)S(1)}, bf16[16,2652]{1,0:T(8,128)(2,1)S(1)}, u32[]{:S(2)}, u32[]{:S(2)}) collective-permute-start(bf16[16,2652]{1,0:T(8,128)(2,1)S(1)} %get-tuple-element.19), channel_id=1, source_target_pairs={{0,8},{8,0},{16,24},{24,16},{1,9},{9,1},{17,25},{25,17},{2,10},{10... | collective-permute-start | bytes 254600 | tf_op jit(solution)/shard_map/ppermute | solution.py:80
  51.0 1.5 %collective-permute-start.18 = (bf16[16,2652]{1,0:T(8,128)(2,1)S(1)}, bf16[16,2652]{1,0:T(8,128)(2,1)S(1)}, u32[]{:S(2)}, u32[]{:S(2)}) collective-permute-start(bf16[16,2652]{1,0:T(8,128)(2,1)S(1)} %get-tuple-element.19), channel_id=1, source_target_pairs={{0,16},{8,24},{16,0},{24,8},{1,17},{9,25},{17,1},{25,9},{2,18},{10... | collective-permute-start | bytes 254600 | tf_op jit(solution)/shard_map/ppermute | solution.py:80
  52.6 1.2 %collective-permute-start.19 = (bf16[16,2652]{1,0:T(8,128)(2,1)S(1)}, bf16[16,2652]{1,0:T(8,128)(2,1)S(1)}, u32[]{:S(2)}, u32[]{:S(2)}) collective-permute-start(bf16[16,2652]{1,0:T(8,128)(2,1)S(1)} %get-tuple-element.19), channel_id=1, source_target_pairs={{0,24},{8,16},{16,8},{24,0},{1,25},{9,17},{17,9},{25,1},{2,26},{10... | collective-permute-start | bytes 254600 | tf_op jit(solution)/shard_map/ppermute | solution.py:80
  53.9 0.4 collective-permute-start.21
  54.3 5.8 %collective-permute-done.18 = bf16[16,2652]{1,0:T(8,128)(2,1)S(1)} collective-permute-done((bf16[16,2652]{1,0:T(8,128)(2,1)S(1)}, bf16[16,2652]{1,0:T(8,128)(2,1)S(1)}, u32[]{:S(2)}, u32[]{:S(2)}) %collective-permute-start.18) | collective-permute-done | bytes 84896 | tf_op jit(solution)/shard_map/ppermute | solution.py:80
  60.2 0.6 collective-permute-start.23
  60.8 0.6 collective-permute-done.22
  61.4 0.2 collective-permute-done.23
  61.7 0.2 convolution_convert_fusion.1
  61.9 0.2 fusion.26
  62.2 0.2 convolution_convert_fusion.2
  62.4 0.5 fusion.14
  62.9 0.2 convolution_convert_fusion.3
  63.1 0.2 fusion.32
  63.4 0.2 convolution_convert_fusion.4
  63.6 0.2 fusion.35
  63.9 1.6 %collective-permute-start.30 = (bf16[48,2652]{1,0:T(8,128)(2,1)S(1)}, bf16[48,2652]{1,0:T(8,128)(2,1)S(1)}, u32[]{:S(2)}, u32[]{:S(2)}) collective-permute-start(bf16[48,2652]{1,0:T(8,128)(2,1)S(1)} %convolution_convert_fusion.1), channel_id=1, source_target_pairs={{0,1},{1,0},{2,3},{3,2},{4,5},{5,4},{6,7},{7,6},{8,9},{9,8},{10,11... | collective-permute-start | bytes 763784 | tf_op jit(solution)/shard_map/ppermute | solution.py:80
  65.4 1.5 %collective-permute-start.28 = (bf16[48,2652]{1,0:T(8,128)(2,1)S(1)}, bf16[48,2652]{1,0:T(8,128)(2,1)S(1)}, u32[]{:S(2)}, u32[]{:S(2)}) collective-permute-start(bf16[48,2652]{1,0:T(8,128)(2,1)S(1)} %convolution_convert_fusion.2), channel_id=1, source_target_pairs={{0,4},{4,0},{1,5},{5,1},{2,6},{6,2},{3,7},{7,3},{8,12},{12,8},{9,1... | collective-permute-start | bytes 763784 | tf_op jit(solution)/shard_map/ppermute | solution.py:80
  66.9 0.5 collective-permute-start.26
  67.4 0.5 collective-permute-start.24
  68.0 0.2 fusion.29
  68.2 4.8 %collective-permute-done.30 = bf16[48,2652]{1,0:T(8,128)(2,1)S(1)} collective-permute-done((bf16[48,2652]{1,0:T(8,128)(2,1)S(1)}, bf16[48,2652]{1,0:T(8,128)(2,1)S(1)}, u32[]{:S(2)}, u32[]{:S(2)}) %collective-permute-start.30) | collective-permute-done | bytes 254624 | tf_op jit(solution)/shard_map/ppermute | solution.py:80
  73.1 1.5 %collective-permute-start.31 = (bf16[24,2652]{1,0:T(8,128)(2,1)S(1)}, bf16[24,2652]{1,0:T(8,128)(2,1)S(1)}, u32[]{:S(2)}, u32[]{:S(2)}) collective-permute-start(bf16[24,2652]{1,0:T(8,128)(2,1)S(1)} %get-tuple-element.24), channel_id=1, source_target_pairs={{0,4},{4,0},{1,5},{5,1},{2,6},{6,2},{3,7},{7,3},{8,12},{12,8},{9,1... | collective-permute-start | bytes 381896 | tf_op jit(solution)/shard_map/ppermute | solution.py:80
  74.6 3.6 %collective-permute-done.26 = bf16[48,2704]{1,0:T(8,128)(2,1)S(1)} collective-permute-done((bf16[48,2704]{1,0:T(8,128)(2,1)S(1)}, bf16[48,2704]{1,0:T(8,128)(2,1)S(1)}, u32[]{:S(2)}, u32[]{:S(2)}) %collective-permute-start.26) | collective-permute-done | bytes 259616 | tf_op jit(solution)/shard_map/ppermute | solution.py:80
  78.3 1.6 %collective-permute-start.27 = (bf16[24,2704]{1,0:T(8,128)(2,1)S(1)}, bf16[24,2704]{1,0:T(8,128)(2,1)S(1)}, u32[]{:S(2)}, u32[]{:S(2)}) collective-permute-start(bf16[24,2704]{1,0:T(8,128)(2,1)S(1)} %get-tuple-element.20), channel_id=1, source_target_pairs={{0,4},{4,0},{1,5},{5,1},{2,6},{6,2},{3,7},{7,3},{8,12},{12,8},{9,1... | collective-permute-start | bytes 389384 | tf_op jit(solution)/shard_map/ppermute | solution.py:80
  79.8 0.5 collective-permute-done.24
  80.4 1.1 %collective-permute-start.25 = (bf16[24,2704]{1,0:T(8,128)(2,1)S(1)}, bf16[24,2704]{1,0:T(8,128)(2,1)S(1)}, u32[]{:S(2)}, u32[]{:S(2)}) collective-permute-start(bf16[24,2704]{1,0:T(8,128)(2,1)S(1)} %get-tuple-element.22), channel_id=1, source_target_pairs={{0,1},{1,0},{2,3},{3,2},{4,5},{5,4},{6,7},{7,6},{8,9},{9,8},{10,11... | collective-permute-start | bytes 389384 | tf_op jit(solution)/shard_map/ppermute | solution.py:80
  81.5 1.1 %collective-permute-start.29 = (bf16[24,2652]{1,0:T(8,128)(2,1)S(1)}, bf16[24,2652]{1,0:T(8,128)(2,1)S(1)}, u32[]{:S(2)}, u32[]{:S(2)}) collective-permute-start(bf16[24,2652]{1,0:T(8,128)(2,1)S(1)} %get-tuple-element.26), channel_id=1, source_target_pairs={{0,1},{1,0},{2,3},{3,2},{4,5},{5,4},{6,7},{7,6},{8,9},{9,8},{10,11... | collective-permute-start | bytes 381896 | tf_op jit(solution)/shard_map/ppermute | solution.py:80
  82.6 0.5 collective-permute-done.31.refs_7_
  83.1 4.3 %collective-permute-done.29.refs_5_ = bf16[24,2652]{1,0:T(8,128)(2,1)S(1)} collective-permute-done((bf16[24,2652]{1,0:T(8,128)(2,1)S(1)}, bf16[24,2652]{1,0:T(8,128)(2,1)S(1)}, u32[]{:S(2)}, u32[]{:S(2)}) %collective-permute-start.29) | collective-permute-done | bytes 127328 | tf_op jit(solution)/shard_map/ppermute | solution.py:80
  87.4 1.6 %shard_map.84 = (f32[48,2704]{1,0:T(8,128)S(1)}, f32[48,2652]{1,0:T(8,128)S(1)}, f32[32,128]{1,0:T(8,128)}) custom-call(f32[24,2704]{1,0:T(8,128)S(1)} %get-tuple-element.23.refs_0_, bf16[24,2704]{1,0:T(8,128)(2,1)S(1)} %collective-permute-done.25.refs_1_, f32[24,2704]{1,0:T(8,128)S(1)} %get-tuple-element.21.refs_2_, ...), custom_call_target="tpu_custom_call" | custom-call | tf_op jit(solution)/shard_map/pallas_call | solution.py:188
  89.0 3.3 %all-to-all-start = ((f32[32,1,128]{2,1,0:T(1,128)}), f32[32,1,128]{2,1,0:T(1,128)S(1)}, u32[]{:S(2)}, u32[]{:S(2)}) async-start(f32[32,1,128]{2,1,0:T(1,128)} %bitcast.4), calls=%async_computation | async-start | bytes 32768 | tf_op jit(solution)/shard_map/all_to_all | solution.py:198
  92.4 0.6 convert_element_type.98
  93.0 6.5 %all-to-all-done = f32[32,1,128]{2,1,0:T(1,128)S(1)} async-done(((f32[32,1,128]{2,1,0:T(1,128)}), f32[32,1,128]{2,1,0:T(1,128)S(1)}, u32[]{:S(2)}, u32[]{:S(2)}) %all-to-all-start) | async-done | bytes 16416 | tf_op jit(solution)/shard_map/all_to_all | solution.py:198
  99.5 1.1 %shard_map.85 = (f32[48,2704]{1,0:T(8,128)}, f32[48,2652]{1,0:T(8,128)}, f32[1]{0:T(128)}) custom-call(f32[32,128]{1,0:T(8,128)S(1)} %bitcast.23, f32[48,2704]{1,0:T(8,128)S(1)} %get-tuple-element.11.grad_in, f32[48,2652]{1,0:T(8,128)S(1)} %get-tuple-element.12.grad_out), custom_call_target="tpu_custom_call" | custom-call | tf_op jit(solution)/shard_map/pallas_call | solution.py:201
  (63 shorter events, 1.1 us)
Async XLA Ops:
  0.6 16.2 %copy-start.2 = (bf16[48,2652]{1,0:T(8,128)(2,1)S(1)}, bf16[48,2652]{1,0:T(8,128)(2,1)}, u32[]{:S(2)}) copy-start(bf16[48,2652]{1,0:T(8,128)(2,1)} %param.9) | copy-start | bytes 763780
  2.4 9.3 %collective-permute-start = (bf16[16,2704]{1,0:T(8,128)(2,1)S(1)}, bf16[16,2704]{1,0:T(8,128)(2,1)S(1)}, u32[]{:S(2)}, u32[]{:S(2)}) collective-permute-start(bf16[16,2704]{1,0:T(8,128)(2,1)S(1)} %get-tuple-element.31), channel_id=1, source_target_pairs={{0,8},{8,0},{16,24},{24,16},{1,9},{9,1},{17,25},{25,17},{2,10},{10... | collective-permute-start | bytes 259592 | tf_op jit(solution)/shard_map/ppermute | solution.py:80
  5.5 9.8 %collective-permute-start.1 = (bf16[16,2704]{1,0:T(8,128)(2,1)S(1)}, bf16[16,2704]{1,0:T(8,128)(2,1)S(1)}, u32[]{:S(2)}, u32[]{:S(2)}) collective-permute-start(bf16[16,2704]{1,0:T(8,128)(2,1)S(1)} %get-tuple-element.31), channel_id=1, source_target_pairs={{0,16},{8,24},{16,0},{24,8},{1,17},{9,25},{17,1},{25,9},{2,18},{10... | collective-permute-start | bytes 259592 | tf_op jit(solution)/shard_map/ppermute | solution.py:80
  8.1 8.7 %collective-permute-start.2 = (bf16[16,2704]{1,0:T(8,128)(2,1)S(1)}, bf16[16,2704]{1,0:T(8,128)(2,1)S(1)}, u32[]{:S(2)}, u32[]{:S(2)}) collective-permute-start(bf16[16,2704]{1,0:T(8,128)(2,1)S(1)} %get-tuple-element.31), channel_id=1, source_target_pairs={{0,24},{8,16},{16,8},{24,0},{1,25},{9,17},{17,9},{25,1},{2,26},{10... | collective-permute-start | bytes 259592 | tf_op jit(solution)/shard_map/ppermute | solution.py:80
  8.1 10.3 %collective-permute-start.3 = (bf16[16,2704]{1,0:T(8,128)(2,1)S(1)}, bf16[16,2704]{1,0:T(8,128)(2,1)S(1)}, u32[]{:S(2)}, u32[]{:S(2)}) collective-permute-start(bf16[16,2704]{1,0:T(8,128)(2,1)S(1)} %get-tuple-element.31), channel_id=1, source_target_pairs={{0,2},{2,0},{1,3},{3,1},{4,6},{6,4},{5,7},{7,5},{8,10},{10,8},{9,1... | collective-permute-start | bytes 259592 | tf_op jit(solution)/shard_map/ppermute | solution.py:80
  8.1 18.4 %collective-permute-start.7 = (bf16[48,2704]{1,0:T(8,128)(2,1)}, bf16[48,2704]{1,0:T(8,128)(2,1)S(1)}, u32[]{:S(2)}, u32[]{:S(2)}) collective-permute-start(bf16[48,2704]{1,0:T(8,128)(2,1)} %param.8), channel_id=1, source_target_pairs={{0,1},{1,0},{2,3},{3,2},{4,5},{5,4},{6,7},{7,6},{8,9},{9,8},{10,11... | collective-permute-start | bytes 778760 | tf_op jit(solution)/shard_map/ppermute | solution.py:80
  11.7 16.6 %collective-permute-start.8 = (bf16[48,2704]{1,0:T(8,128)(2,1)}, bf16[48,2704]{1,0:T(8,128)(2,1)S(1)}, u32[]{:S(2)}, u32[]{:S(2)}) collective-permute-start(bf16[48,2704]{1,0:T(8,128)(2,1)} %param.8), channel_id=1, source_target_pairs={{0,4},{4,0},{1,5},{5,1},{2,6},{6,2},{3,7},{7,3},{8,12},{12,8},{9,1... | collective-permute-start | bytes 778760 | tf_op jit(solution)/shard_map/ppermute | solution.py:80
  15.3 10.8 %collective-permute-start.11 = (bf16[48,2652]{1,0:T(8,128)(2,1)}, bf16[48,2652]{1,0:T(8,128)(2,1)S(1)}, u32[]{:S(2)}, u32[]{:S(2)}) collective-permute-start(bf16[48,2652]{1,0:T(8,128)(2,1)} %param.9), channel_id=1, source_target_pairs={{0,4},{4,0},{1,5},{5,1},{2,6},{6,2},{3,7},{7,3},{8,12},{12,8},{9,1... | collective-permute-start | bytes 763784 | tf_op jit(solution)/shard_map/ppermute | solution.py:80
  16.8 9.6 %collective-permute-start.10 = (bf16[48,2652]{1,0:T(8,128)(2,1)S(1)}, bf16[48,2652]{1,0:T(8,128)(2,1)S(1)}, u32[]{:S(2)}, u32[]{:S(2)}) collective-permute-start(bf16[48,2652]{1,0:T(8,128)(2,1)S(1)} %copy-done.2), channel_id=1, source_target_pairs={{0,1},{1,0},{2,3},{3,2},{4,5},{5,4},{6,7},{7,6},{8,9},{9,8},{10,11... | collective-permute-start | bytes 763784 | tf_op jit(solution)/shard_map/ppermute | solution.py:80
  18.4 1.4 %collective-permute-start.4 = (bf16[16,2704]{1,0:T(8,128)(2,1)S(1)}, bf16[16,2704]{1,0:T(8,128)(2,1)S(1)}, u32[]{:S(2)}, u32[]{:S(2)}) collective-permute-start(bf16[16,2704]{1,0:T(8,128)(2,1)S(1)} %collective-permute-done), channel_id=1, source_target_pairs={{0,2},{2,0},{1,3},{3,1},{4,6},{6,4},{5,7},{7,5},{8,10},{10,8},{9,1... | collective-permute-start | bytes 259592 | tf_op jit(solution)/shard_map/ppermute | solution.py:80
  19.8 1.3 %collective-permute-start.5 = (bf16[16,2704]{1,0:T(8,128)(2,1)S(1)}, bf16[16,2704]{1,0:T(8,128)(2,1)S(1)}, u32[]{:S(2)}, u32[]{:S(2)}) collective-permute-start(bf16[16,2704]{1,0:T(8,128)(2,1)S(1)} %collective-permute-done.1), channel_id=1, source_target_pairs={{0,2},{2,0},{1,3},{3,1},{4,6},{6,4},{5,7},{7,5},{8,10},{10,8},{9,1... | collective-permute-start | bytes 259592 | tf_op jit(solution)/shard_map/ppermute | solution.py:80
  21.0 1.3 %collective-permute-start.6 = (bf16[16,2704]{1,0:T(8,128)(2,1)S(1)}, bf16[16,2704]{1,0:T(8,128)(2,1)S(1)}, u32[]{:S(2)}, u32[]{:S(2)}) collective-permute-start(bf16[16,2704]{1,0:T(8,128)(2,1)S(1)} %collective-permute-done.2), channel_id=1, source_target_pairs={{0,2},{2,0},{1,3},{3,1},{4,6},{6,4},{5,7},{7,5},{8,10},{10,8},{9,1... | collective-permute-start | bytes 259592 | tf_op jit(solution)/shard_map/ppermute | solution.py:80
  26.1 7.5 %collective-permute-start.12 = (bf16[48,2652]{1,0:T(8,128)(2,1)S(1)}, bf16[48,2652]{1,0:T(8,128)(2,1)S(1)}, u32[]{:S(2)}, u32[]{:S(2)}) collective-permute-start(bf16[48,2652]{1,0:T(8,128)(2,1)S(1)} %collective-permute-done.11), channel_id=1, source_target_pairs={{0,1},{1,0},{2,3},{3,2},{4,5},{5,4},{6,7},{7,6},{8,9},{9,8},{10,11... | collective-permute-start | bytes 763784 | tf_op jit(solution)/shard_map/ppermute | solution.py:80
  26.4 7.6 %copy-start.1 = (bf16[48,2704]{1,0:T(8,128)(2,1)S(1)}, bf16[48,2704]{1,0:T(8,128)(2,1)}, u32[]{:S(2)}) copy-start(bf16[48,2704]{1,0:T(8,128)(2,1)} %param.8) | copy-start | bytes 778756
  26.5 7.5 %collective-permute-start.9 = (bf16[48,2704]{1,0:T(8,128)(2,1)S(1)}, bf16[48,2704]{1,0:T(8,128)(2,1)S(1)}, u32[]{:S(2)}, u32[]{:S(2)}) collective-permute-start(bf16[48,2704]{1,0:T(8,128)(2,1)S(1)} %collective-permute-done.7), channel_id=1, source_target_pairs={{0,4},{4,0},{1,5},{5,1},{2,6},{6,2},{3,7},{7,3},{8,12},{12,8},{9,1... | collective-permute-start | bytes 778760 | tf_op jit(solution)/shard_map/ppermute | solution.py:80
  35.0 13.5 %copy-start = (bf16[16,2652]{1,0:T(8,128)(2,1)S(1)}, bf16[16,2652]{1,0:T(8,128)(2,1)}, u32[]{:S(2)}) copy-start(bf16[16,2652]{1,0:T(8,128)(2,1)} %param.7) | copy-start | bytes 254596
  35.0 1.7 %collective-permute-start.13 = (bf16[64,2652]{1,0:T(8,128)(2,1)S(1)}, bf16[64,2652]{1,0:T(8,128)(2,1)S(1)}, u32[]{:S(2)}, u32[]{:S(2)}) collective-permute-start(bf16[64,2652]{1,0:T(8,128)(2,1)S(1)} %convolution_convert_fusion), channel_id=1, source_target_pairs={{0,2},{2,0},{1,3},{3,1},{4,6},{6,4},{5,7},{7,5},{8,10},{10,8},{9,1... | collective-permute-start | bytes 1018376 | tf_op jit(solution)/shard_map/ppermute | solution.py:80
  37.1 4.6 %collective-permute-start.14 = (bf16[16,2652]{1,0:T(8,128)(2,1)S(1)}, bf16[16,2652]{1,0:T(8,128)(2,1)S(1)}, u32[]{:S(2)}, u32[]{:S(2)}) collective-permute-start(bf16[16,2652]{1,0:T(8,128)(2,1)S(1)} %get-tuple-element.28), channel_id=1, source_target_pairs={{0,8},{8,0},{16,24},{24,16},{1,9},{9,1},{17,25},{25,17},{2,10},{10... | collective-permute-start | bytes 254600 | tf_op jit(solution)/shard_map/ppermute | solution.py:80
  38.1 10.4 %collective-permute-start.15 = (bf16[16,2652]{1,0:T(8,128)(2,1)S(1)}, bf16[16,2652]{1,0:T(8,128)(2,1)S(1)}, u32[]{:S(2)}, u32[]{:S(2)}) collective-permute-start(bf16[16,2652]{1,0:T(8,128)(2,1)S(1)} %get-tuple-element.30), channel_id=1, source_target_pairs={{0,16},{8,24},{16,0},{24,8},{1,17},{9,25},{17,1},{25,9},{2,18},{10... | collective-permute-start | bytes 254600 | tf_op jit(solution)/shard_map/ppermute | solution.py:80
  41.5 6.9 %collective-permute-start.16 = (bf16[16,2652]{1,0:T(8,128)(2,1)S(1)}, bf16[16,2652]{1,0:T(8,128)(2,1)S(1)}, u32[]{:S(2)}, u32[]{:S(2)}) collective-permute-start(bf16[16,2652]{1,0:T(8,128)(2,1)S(1)} %get-tuple-element.29), channel_id=1, source_target_pairs={{0,24},{8,16},{16,8},{24,0},{1,25},{9,17},{17,9},{25,1},{2,26},{10... | collective-permute-start | bytes 254600 | tf_op jit(solution)/shard_map/ppermute | solution.py:80
  49.2 4.7 %collective-permute-start.17 = (bf16[16,2652]{1,0:T(8,128)(2,1)S(1)}, bf16[16,2652]{1,0:T(8,128)(2,1)S(1)}, u32[]{:S(2)}, u32[]{:S(2)}) collective-permute-start(bf16[16,2652]{1,0:T(8,128)(2,1)S(1)} %get-tuple-element.19), channel_id=1, source_target_pairs={{0,8},{8,0},{16,24},{24,16},{1,9},{9,1},{17,25},{25,17},{2,10},{10... | collective-permute-start | bytes 254600 | tf_op jit(solution)/shard_map/ppermute | solution.py:80
  51.0 9.1 %collective-permute-start.18 = (bf16[16,2652]{1,0:T(8,128)(2,1)S(1)}, bf16[16,2652]{1,0:T(8,128)(2,1)S(1)}, u32[]{:S(2)}, u32[]{:S(2)}) collective-permute-start(bf16[16,2652]{1,0:T(8,128)(2,1)S(1)} %get-tuple-element.19), channel_id=1, source_target_pairs={{0,16},{8,24},{16,0},{24,8},{1,17},{9,25},{17,1},{25,9},{2,18},{10... | collective-permute-start | bytes 254600 | tf_op jit(solution)/shard_map/ppermute | solution.py:80
  52.6 7.6 %collective-permute-start.19 = (bf16[16,2652]{1,0:T(8,128)(2,1)S(1)}, bf16[16,2652]{1,0:T(8,128)(2,1)S(1)}, u32[]{:S(2)}, u32[]{:S(2)}) collective-permute-start(bf16[16,2652]{1,0:T(8,128)(2,1)S(1)} %get-tuple-element.19), channel_id=1, source_target_pairs={{0,24},{8,16},{16,8},{24,0},{1,25},{9,17},{17,9},{25,1},{2,26},{10... | collective-permute-start | bytes 254600 | tf_op jit(solution)/shard_map/ppermute | solution.py:80
  53.8 7.0 %collective-permute-start.20 = (bf16[16,2652]{1,0:T(8,128)(2,1)S(1)}, bf16[16,2652]{1,0:T(8,128)(2,1)S(1)}, u32[]{:S(2)}, u32[]{:S(2)}) collective-permute-start(bf16[16,2652]{1,0:T(8,128)(2,1)S(1)} %get-tuple-element.19), channel_id=1, source_target_pairs={{0,2},{2,0},{1,3},{3,1},{4,6},{6,4},{5,7},{7,5},{8,10},{10,8},{9,1... | collective-permute-start | bytes 254600 | tf_op jit(solution)/shard_map/ppermute | solution.py:80
  53.9 6.9 %collective-permute-start.21 = (bf16[16,2652]{1,0:T(8,128)(2,1)S(1)}, bf16[16,2652]{1,0:T(8,128)(2,1)S(1)}, u32[]{:S(2)}, u32[]{:S(2)}) collective-permute-start(bf16[16,2652]{1,0:T(8,128)(2,1)S(1)} %collective-permute-done.17), channel_id=1, source_target_pairs={{0,2},{2,0},{1,3},{3,1},{4,6},{6,4},{5,7},{7,5},{8,10},{10,8},{9,1... | collective-permute-start | bytes 254600 | tf_op jit(solution)/shard_map/ppermute | solution.py:80
  60.1 1.3 %collective-permute-start.22 = (bf16[16,2652]{1,0:T(8,128)(2,1)S(1)}, bf16[16,2652]{1,0:T(8,128)(2,1)S(1)}, u32[]{:S(2)}, u32[]{:S(2)}) collective-permute-start(bf16[16,2652]{1,0:T(8,128)(2,1)S(1)} %collective-permute-done.18), channel_id=1, source_target_pairs={{0,2},{2,0},{1,3},{3,1},{4,6},{6,4},{5,7},{7,5},{8,10},{10,8},{9,1... | collective-permute-start | bytes 254600 | tf_op jit(solution)/shard_map/ppermute | solution.py:80
  60.2 1.5 %collective-permute-start.23 = (bf16[16,2652]{1,0:T(8,128)(2,1)S(1)}, bf16[16,2652]{1,0:T(8,128)(2,1)S(1)}, u32[]{:S(2)}, u32[]{:S(2)}) collective-permute-start(bf16[16,2652]{1,0:T(8,128)(2,1)S(1)} %collective-permute-done.19), channel_id=1, source_target_pairs={{0,2},{2,0},{1,3},{3,1},{4,6},{6,4},{5,7},{7,5},{8,10},{10,8},{9,1... | collective-permute-start | bytes 254600 | tf_op jit(solution)/shard_map/ppermute | solution.py:80
  63.9 9.2 %collective-permute-start.30 = (bf16[48,2652]{1,0:T(8,128)(2,1)S(1)}, bf16[48,2652]{1,0:T(8,128)(2,1)S(1)}, u32[]{:S(2)}, u32[]{:S(2)}) collective-permute-start(bf16[48,2652]{1,0:T(8,128)(2,1)S(1)} %convolution_convert_fusion.1), channel_id=1, source_target_pairs={{0,1},{1,0},{2,3},{3,2},{4,5},{5,4},{6,7},{7,6},{8,9},{9,8},{10,11... | collective-permute-start | bytes 763784 | tf_op jit(solution)/shard_map/ppermute | solution.py:80
  65.4 16.0 %collective-permute-start.28 = (bf16[48,2652]{1,0:T(8,128)(2,1)S(1)}, bf16[48,2652]{1,0:T(8,128)(2,1)S(1)}, u32[]{:S(2)}, u32[]{:S(2)}) collective-permute-start(bf16[48,2652]{1,0:T(8,128)(2,1)S(1)} %convolution_convert_fusion.2), channel_id=1, source_target_pairs={{0,4},{4,0},{1,5},{5,1},{2,6},{6,2},{3,7},{7,3},{8,12},{12,8},{9,1... | collective-permute-start | bytes 763784 | tf_op jit(solution)/shard_map/ppermute | solution.py:80
  66.9 11.3 %collective-permute-start.26 = (bf16[48,2704]{1,0:T(8,128)(2,1)S(1)}, bf16[48,2704]{1,0:T(8,128)(2,1)S(1)}, u32[]{:S(2)}, u32[]{:S(2)}) collective-permute-start(bf16[48,2704]{1,0:T(8,128)(2,1)S(1)} %convolution_convert_fusion.3), channel_id=1, source_target_pairs={{0,1},{1,0},{2,3},{3,2},{4,5},{5,4},{6,7},{7,6},{8,9},{9,8},{10,11... | collective-permute-start | bytes 778760 | tf_op jit(solution)/shard_map/ppermute | solution.py:80
  67.4 12.9 %collective-permute-start.24 = (bf16[48,2704]{1,0:T(8,128)(2,1)S(1)}, bf16[48,2704]{1,0:T(8,128)(2,1)S(1)}, u32[]{:S(2)}, u32[]{:S(2)}) collective-permute-start(bf16[48,2704]{1,0:T(8,128)(2,1)S(1)} %convolution_convert_fusion.4), channel_id=1, source_target_pairs={{0,4},{4,0},{1,5},{5,1},{2,6},{6,2},{3,7},{7,3},{8,12},{12,8},{9,1... | collective-permute-start | bytes 778760 | tf_op jit(solution)/shard_map/ppermute | solution.py:80
  73.1 10.0 %collective-permute-start.31 = (bf16[24,2652]{1,0:T(8,128)(2,1)S(1)}, bf16[24,2652]{1,0:T(8,128)(2,1)S(1)}, u32[]{:S(2)}, u32[]{:S(2)}) collective-permute-start(bf16[24,2652]{1,0:T(8,128)(2,1)S(1)} %get-tuple-element.24), channel_id=1, source_target_pairs={{0,4},{4,0},{1,5},{5,1},{2,6},{6,2},{3,7},{7,3},{8,12},{12,8},{9,1... | collective-permute-start | bytes 381896 | tf_op jit(solution)/shard_map/ppermute | solution.py:80
  78.3 9.2 %collective-permute-start.27 = (bf16[24,2704]{1,0:T(8,128)(2,1)S(1)}, bf16[24,2704]{1,0:T(8,128)(2,1)S(1)}, u32[]{:S(2)}, u32[]{:S(2)}) collective-permute-start(bf16[24,2704]{1,0:T(8,128)(2,1)S(1)} %get-tuple-element.20), channel_id=1, source_target_pairs={{0,4},{4,0},{1,5},{5,1},{2,6},{6,2},{3,7},{7,3},{8,12},{12,8},{9,1... | collective-permute-start | bytes 389384 | tf_op jit(solution)/shard_map/ppermute | solution.py:80
  80.4 7.0 %collective-permute-start.25 = (bf16[24,2704]{1,0:T(8,128)(2,1)S(1)}, bf16[24,2704]{1,0:T(8,128)(2,1)S(1)}, u32[]{:S(2)}, u32[]{:S(2)}) collective-permute-start(bf16[24,2704]{1,0:T(8,128)(2,1)S(1)} %get-tuple-element.22), channel_id=1, source_target_pairs={{0,1},{1,0},{2,3},{3,2},{4,5},{5,4},{6,7},{7,6},{8,9},{9,8},{10,11... | collective-permute-start | bytes 389384 | tf_op jit(solution)/shard_map/ppermute | solution.py:80
  81.5 5.9 %collective-permute-start.29 = (bf16[24,2652]{1,0:T(8,128)(2,1)S(1)}, bf16[24,2652]{1,0:T(8,128)(2,1)S(1)}, u32[]{:S(2)}, u32[]{:S(2)}) collective-permute-start(bf16[24,2652]{1,0:T(8,128)(2,1)S(1)} %get-tuple-element.26), channel_id=1, source_target_pairs={{0,1},{1,0},{2,3},{3,2},{4,5},{5,4},{6,7},{7,6},{8,9},{9,8},{10,11... | collective-permute-start | bytes 381896 | tf_op jit(solution)/shard_map/ppermute | solution.py:80
  89.0 10.5 %all-to-all-start = ((f32[32,1,128]{2,1,0:T(1,128)}), f32[32,1,128]{2,1,0:T(1,128)S(1)}, u32[]{:S(2)}, u32[]{:S(2)}) async-start(f32[32,1,128]{2,1,0:T(1,128)} %bitcast.4), calls=%async_computation | async-start | bytes 32768 | tf_op jit(solution)/shard_map/all_to_all | solution.py:198
where the time goes:
time: 101 us
  waiting for transfers between devices  50.5 us (50%)
  starting transfers between devices  37.2 us (37%)
  matrix products  3.6 us (4%)
  other arithmetic  3.42 us (3%)
  Pallas kernels  2.76 us (3%)
  local copies, waits for them, and re-layouts  2.24 us (2%)
    ppermute x32, waiting for transfers between devices, exchange(): lax.ppermute(block, axes, [(index, index ^ step) for index in range(count)])  44 us
    ppermute x32, starting transfers between devices, exchange(): lax.ppermute(block, axes, [(index, index ^ step) for index in range(count)])  33.8 us
    all_to_all x1, waiting for transfers between devices, torus_body(): lax.all_to_all(copies, ('z', 'x', 'c', 'y'), split_axis=0, concat_axis=0,...  6.5 us
    all_to_all x1, starting transfers between devices, torus_body(): lax.all_to_all(copies, ('z', 'x', 'c', 'y'), split_axis=0, concat_axis=0,...  3.35 us
    unnamed x32, local copies, waits for them, and re-layouts  2.17 us
  transfers between devices with their start and end apart: 33, of which 20 were waited for; matrix products, arithmetic and copies ran while one was open for 3% of the time, Pallas kernels for 0%

commit v1 on v0

--- a/solution.py
+++ b/solution.py
@@ -92,10 +92,16 @@
     far = []
     for block in near:
         far.append(exchange(block, ("c",), 1))
-    return jnp.concatenate(near + far, axis=0)
-
-
-def gather_units(w_in, w_out):
+    return near + far
+
+
+def order_units(own, along_x, along_y, diagonal):
+    own, along_x, along_y, diagonal = (split_rows(rows, 2) for rows in (own, along_x, along_y, diagonal))
+    first = [own[0], along_y[0], along_x[0], diagonal[0]]
+    return jnp.concatenate(first + [own[1], along_x[1], along_y[1], diagonal[1]], axis=0)
+
+
+def gather_inputs(w_in, w_out, features):
     in_y = exchange(w_in, ("y",), 1)
     out_x = exchange(w_out, ("x",), 1)
     in_x = exchange(w_in, ("x",), 1)
@@ -103,12 +109,11 @@
     in_xy = exchange(in_y, ("x",), 1)
     out_xy = exchange(out_x, ("y",), 1)
 
-    def ordered(own, along_x, along_y, diagonal):
-        own, along_x, along_y, diagonal = (split_rows(rows, 2) for rows in (own, along_x, along_y, diagonal))
-        first = [own[0], along_y[0], along_x[0], diagonal[0]]
-        return jnp.concatenate(first + [own[1], along_x[1], along_y[1], diagonal[1]], axis=0)
-
-    return ordered(w_in, in_x, in_y, in_xy), ordered(w_out, out_x, out_y, out_xy)
+    states = gather_states(features)
+    in_x, out_y, *states = lax.optimization_barrier((in_x, out_y, *states))
+    units_in = order_units(w_in, in_x, in_y, in_xy)
+    units_out = order_units(w_out, out_x, out_y, out_xy)
+    return units_in, units_out, jnp.concatenate(states, axis=0)
 
 
 def plane_sum(left, right):
@@ -161,8 +166,7 @@
     device_count = z_count * lax.axis_size(("x", "y", "c"))
     stored_rows = ranges.shape[0]
     value_width = w_out.shape[1]
-    units_in, units_out = gather_units(w_in, w_out)
-    features = gather_states(build_features(ranges, board))
+    units_in, units_out, features = gather_inputs(w_in, w_out, build_features(ranges, board))
     preact = right_product(features, units_in)
     hidden = jax.nn.gelu(preact).astype(jnp.bfloat16)
     own_hidden, other_hidden = split_rows(hidden, 2)
@@ -171,11 +175,10 @@
     own_value = jnp.dot(own_hidden, units_out, preferred_element_type=jnp.float32)
     chip_value = split_rows(own_value + other_got.astype(jnp.float32), z_count)
     summed = chip_value[0]
-    received = [exchange(chip_value[k].astype(jnp.bfloat16), ("z",), k) for k in range(1, z_count)]
-    for part in received:
-        summed = summed + part.astype(jnp.float32)
+    for step in range(1, z_count):
+        summed = summed + exchange(chip_value[step].astype(jnp.bfloat16), ("z",), step).astype(jnp.float32)
     error_value = summed - targets.astype(jnp.float32)
-    out_grad = gather_states(jnp.clip(error_value, -1.0, 1.0).astype(jnp.bfloat16))
+    out_grad = jnp.concatenate(gather_states(jnp.clip(error_value, -1.0, 1.0).astype(jnp.bfloat16)), axis=0)
     predicted = summed.astype(jnp.bfloat16)
     loss_part = jnp.sum(huber_terms(error_value))
     parts_out = plane_sum(hidden, out_grad)

time: 101 us -> 101 us (level)
  waiting for transfers between devices: 50.5 us -> 53.2 us
  starting transfers between devices: 37.2 us -> 34.9 us
    ppermute x32, waiting for transfers between devices: 44 us -> 46.7 us  [exchange(): lax.ppermute(block, axes, [(index, index ^ step) for index in range(count)])]
    ppermute x32, starting transfers between devices: 33.8 us -> 31.3 us  [exchange(): lax.ppermute(block, axes, [(index, index ^ step) for index in range(count)])]
    unnamed x32 -> x33, local copies, waits for them, and re-layouts: 2.17 us -> 2.15 us
  transfers between devices with their start and end apart: 33 -> 33, of which waited for: 20 -> 18; matrix products, arithmetic and copies ran while one was open for 3% -> 3% of each run, Pallas kernels for 0% -> 0%
where the time goes in v1:
time: 101 us
  waiting for transfers between devices  53.2 us (53%)
  starting transfers between devices  34.9 us (35%)
  matrix products  3.59 us (4%)
  other arithmetic  3.37 us (3%)
  Pallas kernels  2.76 us (3%)
  local copies, waits for them, and re-layouts  2.22 us (2%)
    ppermute x32, waiting for transfers between devices, exchange(): lax.ppermute(block, axes, [(index, index ^ step) for index in range(count)])  46.7 us
    ppermute x32, starting transfers between devices, exchange(): lax.ppermute(block, axes, [(index, index ^ step) for index in range(count)])  31.3 us
    all_to_all x1, waiting for transfers between devices, torus_body(): lax.all_to_all(copies, ('z', 'x', 'c', 'y'), split_axis=0, concat_axis=0,...  6.5 us
    all_to_all x1, starting transfers between devices, torus_body(): lax.all_to_all(copies, ('z', 'x', 'c', 'y'), split_axis=0, concat_axis=0,...  3.65 us
    unnamed x33, local copies, waits for them, and re-layouts  2.15 us
  transfers between devices with their start and end apart: 33, of which 18 were waited for; matrix products, arithmetic and copies ran while one was open for 3% of the time, Pallas kernels for 0%

profile of v1, /device:TPU:0, one launch (start us, length us, event | category | flops | bytes accessed | tf_op | source)
XLA Modules:
  0.0 101.0 jit_solution(8585701052742259000)
XLA Ops:
  0.6 0.8 convert_reduce_fusion
  1.4 1.0 pad_maximum_fusion
  2.4 3.1 %collective-permute-start.2 = (bf16[16,2704]{1,0:T(8,128)(2,1)S(1)}, bf16[16,2704]{1,0:T(8,128)(2,1)S(1)}, u32[]{:S(2)}, u32[]{:S(2)}) collective-permute-start(bf16[16,2704]{1,0:T(8,128)(2,1)S(1)} %pad_maximum_fusion), channel_id=1, source_target_pairs={{0,8},{8,0},{16,24},{24,16},{1,9},{9,1},{17,25},{25,17},{2,10},{10... | collective-permute-start | bytes 259592 | tf_op jit(solution)/shard_map/ppermute | solution.py:80
  5.4 2.6 %collective-permute-start.3 = (bf16[16,2704]{1,0:T(8,128)(2,1)S(1)}, bf16[16,2704]{1,0:T(8,128)(2,1)S(1)}, u32[]{:S(2)}, u32[]{:S(2)}) collective-permute-start(bf16[16,2704]{1,0:T(8,128)(2,1)S(1)} %pad_maximum_fusion), channel_id=1, source_target_pairs={{0,16},{8,24},{16,0},{24,8},{1,17},{9,25},{17,1},{25,9},{2,18},{10... | collective-permute-start | bytes 259592 | tf_op jit(solution)/shard_map/ppermute | solution.py:80
  8.0 1.7 %collective-permute-start = (bf16[48,2704]{1,0:T(8,128)(2,1)}, bf16[48,2704]{1,0:T(8,128)(2,1)S(1)}, u32[]{:S(2)}, u32[]{:S(2)}) collective-permute-start(bf16[48,2704]{1,0:T(8,128)(2,1)} %param.8), channel_id=1, source_target_pairs={{0,4},{4,0},{1,5},{5,1},{2,6},{6,2},{3,7},{7,3},{8,12},{12,8},{9,1... | collective-permute-start | bytes 778760 | tf_op jit(solution)/shard_map/ppermute | solution.py:80
  9.7 0.2 collective-permute-start.6
  10.0 0.9 slice_dynamic-update-slice_fusion.7
  10.9 4.3 %collective-permute-done.3 = bf16[16,2704]{1,0:T(8,128)(2,1)S(1)} collective-permute-done((bf16[16,2704]{1,0:T(8,128)(2,1)S(1)}, bf16[16,2704]{1,0:T(8,128)(2,1)S(1)}, u32[]{:S(2)}, u32[]{:S(2)}) %collective-permute-start.3) | collective-permute-done | bytes 86560 | tf_op jit(solution)/shard_map/ppermute | solution.py:80
  15.2 1.5 %collective-permute-start.1 = (bf16[48,2652]{1,0:T(8,128)(2,1)}, bf16[48,2652]{1,0:T(8,128)(2,1)S(1)}, u32[]{:S(2)}, u32[]{:S(2)}) collective-permute-start(bf16[48,2652]{1,0:T(8,128)(2,1)} %param.9), channel_id=1, source_target_pairs={{0,1},{1,0},{2,3},{3,2},{4,5},{5,4},{6,7},{7,6},{8,9},{9,8},{10,11... | collective-permute-start | bytes 763784 | tf_op jit(solution)/shard_map/ppermute | solution.py:80
  16.8 1.5 %collective-permute-start.11 = (bf16[48,2652]{1,0:T(8,128)(2,1)}, bf16[48,2652]{1,0:T(8,128)(2,1)S(1)}, u32[]{:S(2)}, u32[]{:S(2)}) collective-permute-start(bf16[48,2652]{1,0:T(8,128)(2,1)} %param.9), channel_id=1, source_target_pairs={{0,4},{4,0},{1,5},{5,1},{2,6},{6,2},{3,7},{7,3},{8,12},{12,8},{9,1... | collective-permute-start | bytes 763784 | tf_op jit(solution)/shard_map/ppermute | solution.py:80
  18.3 0.5 collective-permute-start.8
  18.8 0.9 slice_dynamic-update-slice_fusion.15
  19.7 0.6 collective-permute-start.9
  20.3 3.0 %collective-permute-done.11 = bf16[48,2652]{1,0:T(8,128)(2,1)S(1)} collective-permute-done((bf16[48,2652]{1,0:T(8,128)(2,1)}, bf16[48,2652]{1,0:T(8,128)(2,1)S(1)}, u32[]{:S(2)}, u32[]{:S(2)}) %collective-permute-start.11) | collective-permute-done | bytes 254624 | tf_op jit(solution)/shard_map/ppermute | solution.py:80
  23.3 1.1 %collective-permute-start.12 = (bf16[48,2652]{1,0:T(8,128)(2,1)S(1)}, bf16[48,2652]{1,0:T(8,128)(2,1)S(1)}, u32[]{:S(2)}, u32[]{:S(2)}) collective-permute-start(bf16[48,2652]{1,0:T(8,128)(2,1)S(1)} %collective-permute-done.11), channel_id=1, source_target_pairs={{0,1},{1,0},{2,3},{3,2},{4,5},{5,4},{6,7},{7,6},{8,9},{9,8},{10,11... | collective-permute-start | bytes 763784 | tf_op jit(solution)/shard_map/ppermute | solution.py:80
  24.5 4.8 %collective-permute-done.9 = bf16[48,2704]{1,0:T(8,128)(2,1)S(1)} collective-permute-done((bf16[48,2704]{1,0:T(8,128)(2,1)}, bf16[48,2704]{1,0:T(8,128)(2,1)S(1)}, u32[]{:S(2)}, u32[]{:S(2)}) %collective-permute-start.9) | collective-permute-done | bytes 259616 | tf_op jit(solution)/shard_map/ppermute | solution.py:80
  29.4 0.6 collective-permute-start.10
  30.0 3.9 %collective-permute-done.12 = bf16[48,2652]{1,0:T(8,128)(2,1)S(1)} collective-permute-done((bf16[48,2652]{1,0:T(8,128)(2,1)S(1)}, bf16[48,2652]{1,0:T(8,128)(2,1)S(1)}, u32[]{:S(2)}, u32[]{:S(2)}) %collective-permute-start.12) | collective-permute-done | bytes 254624 | tf_op jit(solution)/shard_map/ppermute | solution.py:80
  34.1 2.1 %collective-permute-done.10 = bf16[48,2704]{1,0:T(8,128)(2,1)S(1)} collective-permute-done((bf16[48,2704]{1,0:T(8,128)(2,1)S(1)}, bf16[48,2704]{1,0:T(8,128)(2,1)S(1)}, u32[]{:S(2)}, u32[]{:S(2)}) %collective-permute-start.10) | collective-permute-done | bytes 259616 | tf_op jit(solution)/shard_map/ppermute | solution.py:80
  36.3 0.5 multiply_convert_fusion
  36.7 0.4 convolution_convert_fusion
  37.2 1.6 %collective-permute-done.13 = bf16[64,2652]{1,0:T(8,128)(2,1)S(1)} collective-permute-done((bf16[64,2652]{1,0:T(8,128)(2,1)S(1)}, bf16[64,2652]{1,0:T(8,128)(2,1)S(1)}, u32[]{:S(2)}, u32[]{:S(2)}) %collective-permute-start.13) | collective-permute-done | bytes 339488 | tf_op jit(solution)/shard_map/ppermute | solution.py:80
  38.9 0.3 fusion.39
  39.3 3.0 %collective-permute-start.15 = (bf16[16,2652]{1,0:T(8,128)(2,1)S(1)}, bf16[16,2652]{1,0:T(8,128)(2,1)S(1)}, u32[]{:S(2)}, u32[]{:S(2)}) collective-permute-start(bf16[16,2652]{1,0:T(8,128)(2,1)S(1)} %get-tuple-element.50), channel_id=1, source_target_pairs={{0,16},{8,24},{16,0},{24,8},{1,17},{9,25},{17,1},{25,9},{2,18},{10... | collective-permute-start | bytes 254600 | tf_op jit(solution)/shard_map/ppermute | solution.py:80
  42.3 1.3 %collective-permute-start.16 = (bf16[16,2652]{1,0:T(8,128)(2,1)S(1)}, bf16[16,2652]{1,0:T(8,128)(2,1)S(1)}, u32[]{:S(2)}, u32[]{:S(2)}) collective-permute-start(bf16[16,2652]{1,0:T(8,128)(2,1)S(1)} %get-tuple-element.49), channel_id=1, source_target_pairs={{0,24},{8,16},{16,8},{24,0},{1,25},{9,17},{17,9},{25,1},{2,26},{10... | collective-permute-start | bytes 254600 | tf_op jit(solution)/shard_map/ppermute | solution.py:80
  43.7 1.6 %collective-permute-done.14 = bf16[16,2652]{1,0:T(8,128)(2,1)S(1)} collective-permute-done((bf16[16,2652]{1,0:T(8,128)(2,1)S(1)}, bf16[16,2652]{1,0:T(8,128)(2,1)S(1)}, u32[]{:S(2)}, u32[]{:S(2)}) %collective-permute-start.14) | collective-permute-done | bytes 84896 | tf_op jit(solution)/shard_map/ppermute | solution.py:80
  45.2 4.1 %collective-permute-done.15 = bf16[16,2652]{1,0:T(8,128)(2,1)S(1)} collective-permute-done((bf16[16,2652]{1,0:T(8,128)(2,1)S(1)}, bf16[16,2652]{1,0:T(8,128)(2,1)S(1)}, u32[]{:S(2)}, u32[]{:S(2)}) %collective-permute-start.15) | collective-permute-done | bytes 84896 | tf_op jit(solution)/shard_map/ppermute | solution.py:80
  49.3 0.7 fusion.5
  50.1 1.7 %collective-permute-start.17 = (bf16[16,2652]{1,0:T(8,128)(2,1)S(1)}, bf16[16,2652]{1,0:T(8,128)(2,1)S(1)}, u32[]{:S(2)}, u32[]{:S(2)}) collective-permute-start(bf16[16,2652]{1,0:T(8,128)(2,1)S(1)} %get-tuple-element.39), channel_id=1, source_target_pairs={{0,8},{8,0},{16,24},{24,16},{1,9},{9,1},{17,25},{25,17},{2,10},{10... | collective-permute-start | bytes 254600 | tf_op jit(solution)/shard_map/ppermute | solution.py:80
  51.9 1.5 %collective-permute-start.18 = (bf16[16,2652]{1,0:T(8,128)(2,1)S(1)}, bf16[16,2652]{1,0:T(8,128)(2,1)S(1)}, u32[]{:S(2)}, u32[]{:S(2)}) collective-permute-start(bf16[16,2652]{1,0:T(8,128)(2,1)S(1)} %get-tuple-element.39), channel_id=1, source_target_pairs={{0,16},{8,24},{16,0},{24,8},{1,17},{9,25},{17,1},{25,9},{2,18},{10... | collective-permute-start | bytes 254600 | tf_op jit(solution)/shard_map/ppermute | solution.py:80
  53.4 1.3 %collective-permute-start.19 = (bf16[16,2652]{1,0:T(8,128)(2,1)S(1)}, bf16[16,2652]{1,0:T(8,128)(2,1)S(1)}, u32[]{:S(2)}, u32[]{:S(2)}) collective-permute-start(bf16[16,2652]{1,0:T(8,128)(2,1)S(1)} %get-tuple-element.39), channel_id=1, source_target_pairs={{0,24},{8,16},{16,8},{24,0},{1,25},{9,17},{17,9},{25,1},{2,26},{10... | collective-permute-start | bytes 254600 | tf_op jit(solution)/shard_map/ppermute | solution.py:80
  54.6 0.1 collective-permute-done.17
  54.7 0.4 collective-permute-start.21
  55.2 5.8 %collective-permute-done.18 = bf16[16,2652]{1,0:T(8,128)(2,1)S(1)} collective-permute-done((bf16[16,2652]{1,0:T(8,128)(2,1)S(1)}, bf16[16,2652]{1,0:T(8,128)(2,1)S(1)}, u32[]{:S(2)}, u32[]{:S(2)}) %collective-permute-start.18) | collective-permute-done | bytes 84896 | tf_op jit(solution)/shard_map/ppermute | solution.py:80
  61.0 0.6 collective-permute-start.23
  61.6 0.6 collective-permute-done.22
  62.3 0.2 collective-permute-done.23
  62.5 0.2 convolution_convert_fusion.1
  62.7 0.2 fusion.26
  63.0 0.2 convolution_convert_fusion.2
  63.2 0.5 fusion.14
  63.7 0.2 convolution_convert_fusion.3
  63.9 0.2 fusion.32
  64.2 0.2 convolution_convert_fusion.4
  64.4 0.2 fusion.35
  64.7 1.1 %collective-permute-start.30 = (bf16[48,2652]{1,0:T(8,128)(2,1)S(1)}, bf16[48,2652]{1,0:T(8,128)(2,1)S(1)}, u32[]{:S(2)}, u32[]{:S(2)}) collective-permute-start(bf16[48,2652]{1,0:T(8,128)(2,1)S(1)} %convolution_convert_fusion.1), channel_id=1, source_target_pairs={{0,1},{1,0},{2,3},{3,2},{4,5},{5,4},{6,7},{7,6},{8,9},{9,8},{10,11... | collective-permute-start | bytes 763784 | tf_op jit(solution)/shard_map/ppermute | solution.py:80
  65.8 1.1 %collective-permute-start.28 = (bf16[48,2652]{1,0:T(8,128)(2,1)S(1)}, bf16[48,2652]{1,0:T(8,128)(2,1)S(1)}, u32[]{:S(2)}, u32[]{:S(2)}) collective-permute-start(bf16[48,2652]{1,0:T(8,128)(2,1)S(1)} %convolution_convert_fusion.2), channel_id=1, source_target_pairs={{0,4},{4,0},{1,5},{5,1},{2,6},{6,2},{3,7},{7,3},{8,12},{12,8},{9,1... | collective-permute-start | bytes 763784 | tf_op jit(solution)/shard_map/ppermute | solution.py:80
  66.9 0.6 collective-permute-start.26
  67.5 1.3 %collective-permute-start.24 = (bf16[48,2704]{1,0:T(8,128)(2,1)S(1)}, bf16[48,2704]{1,0:T(8,128)(2,1)S(1)}, u32[]{:S(2)}, u32[]{:S(2)}) collective-permute-start(bf16[48,2704]{1,0:T(8,128)(2,1)S(1)} %convolution_convert_fusion.4), channel_id=1, source_target_pairs={{0,4},{4,0},{1,5},{5,1},{2,6},{6,2},{3,7},{7,3},{8,12},{12,8},{9,1... | collective-permute-start | bytes 778760 | tf_op jit(solution)/shard_map/ppermute | solution.py:80
  68.8 0.2 fusion.29
  69.0 4.8 %collective-permute-done.30 = bf16[48,2652]{1,0:T(8,128)(2,1)S(1)} collective-permute-done((bf16[48,2652]{1,0:T(8,128)(2,1)S(1)}, bf16[48,2652]{1,0:T(8,128)(2,1)S(1)}, u32[]{:S(2)}, u32[]{:S(2)}) %collective-permute-start.30) | collective-permute-done | bytes 254624 | tf_op jit(solution)/shard_map/ppermute | solution.py:80
  73.9 0.8 collective-permute-start.31
  74.7 4.3 %collective-permute-done.26 = bf16[48,2704]{1,0:T(8,128)(2,1)S(1)} collective-permute-done((bf16[48,2704]{1,0:T(8,128)(2,1)S(1)}, bf16[48,2704]{1,0:T(8,128)(2,1)S(1)}, u32[]{:S(2)}, u32[]{:S(2)}) %collective-permute-start.26) | collective-permute-done | bytes 259616 | tf_op jit(solution)/shard_map/ppermute | solution.py:80
  79.1 0.8 collective-permute-start.27
  79.9 0.8 collective-permute-done.24
  80.7 1.0 %collective-permute-start.25 = (bf16[24,2704]{1,0:T(8,128)(2,1)S(1)}, bf16[24,2704]{1,0:T(8,128)(2,1)S(1)}, u32[]{:S(2)}, u32[]{:S(2)}) collective-permute-start(bf16[24,2704]{1,0:T(8,128)(2,1)S(1)} %get-tuple-element.42), channel_id=1, source_target_pairs={{0,1},{1,0},{2,3},{3,2},{4,5},{5,4},{6,7},{7,6},{8,9},{9,8},{10,11... | collective-permute-start | bytes 389384 | tf_op jit(solution)/shard_map/ppermute | solution.py:80
  81.8 1.1 %collective-permute-start.29 = (bf16[24,2652]{1,0:T(8,128)(2,1)S(1)}, bf16[24,2652]{1,0:T(8,128)(2,1)S(1)}, u32[]{:S(2)}, u32[]{:S(2)}) collective-permute-start(bf16[24,2652]{1,0:T(8,128)(2,1)S(1)} %get-tuple-element.46), channel_id=1, source_target_pairs={{0,1},{1,0},{2,3},{3,2},{4,5},{5,4},{6,7},{7,6},{8,9},{9,8},{10,11... | collective-permute-start | bytes 381896 | tf_op jit(solution)/shard_map/ppermute | solution.py:80
  83.0 0.5 collective-permute-done.31.refs_7_
  83.4 4.0 %collective-permute-done.29.refs_5_ = bf16[24,2652]{1,0:T(8,128)(2,1)S(1)} collective-permute-done((bf16[24,2652]{1,0:T(8,128)(2,1)S(1)}, bf16[24,2652]{1,0:T(8,128)(2,1)S(1)}, u32[]{:S(2)}, u32[]{:S(2)}) %collective-permute-start.29) | collective-permute-done | bytes 127328 | tf_op jit(solution)/shard_map/ppermute | solution.py:80
  87.5 1.6 %shard_map.84 = (f32[48,2704]{1,0:T(8,128)S(1)}, f32[48,2652]{1,0:T(8,128)S(1)}, f32[32,128]{1,0:T(8,128)}) custom-call(f32[24,2704]{1,0:T(8,128)S(1)} %get-tuple-element.43.refs_0_, bf16[24,2704]{1,0:T(8,128)(2,1)S(1)} %collective-permute-done.25.refs_1_, f32[24,2704]{1,0:T(8,128)S(1)} %get-tuple-element.41.refs_2_, ...), custom_call_target="tpu_custom_call" | custom-call | tf_op jit(solution)/shard_map/pallas_call | solution.py:191
  89.1 3.6 %all-to-all-start = ((f32[32,1,128]{2,1,0:T(1,128)}), f32[32,1,128]{2,1,0:T(1,128)S(1)}, u32[]{:S(2)}, u32[]{:S(2)}) async-start(f32[32,1,128]{2,1,0:T(1,128)} %bitcast.4), calls=%async_computation | async-start | bytes 32768 | tf_op jit(solution)/shard_map/all_to_all | solution.py:201
  92.7 0.6 convert_element_type.98
  93.4 6.5 %all-to-all-done = f32[32,1,128]{2,1,0:T(1,128)S(1)} async-done(((f32[32,1,128]{2,1,0:T(1,128)}), f32[32,1,128]{2,1,0:T(1,128)S(1)}, u32[]{:S(2)}, u32[]{:S(2)}) %all-to-all-start) | async-done | bytes 16416 | tf_op jit(solution)/shard_map/all_to_all | solution.py:201
  99.9 1.1 %shard_map.85 = (f32[48,2704]{1,0:T(8,128)}, f32[48,2652]{1,0:T(8,128)}, f32[1]{0:T(128)}) custom-call(f32[32,128]{1,0:T(8,128)S(1)} %bitcast.23, f32[48,2704]{1,0:T(8,128)S(1)} %get-tuple-element.31.grad_in, f32[48,2652]{1,0:T(8,128)S(1)} %get-tuple-element.32.grad_out), custom_call_target="tpu_custom_call" | custom-call | tf_op jit(solution)/shard_map/pallas_call | solution.py:204
  (64 shorter events, 0.9 us)
Async XLA Ops:
  2.4 7.4 %collective-permute-start.2 = (bf16[16,2704]{1,0:T(8,128)(2,1)S(1)}, bf16[16,2704]{1,0:T(8,128)(2,1)S(1)}, u32[]{:S(2)}, u32[]{:S(2)}) collective-permute-start(bf16[16,2704]{1,0:T(8,128)(2,1)S(1)} %pad_maximum_fusion), channel_id=1, source_target_pairs={{0,8},{8,0},{16,24},{24,16},{1,9},{9,1},{17,25},{25,17},{2,10},{10... | collective-permute-start | bytes 259592 | tf_op jit(solution)/shard_map/ppermute | solution.py:80
  5.4 9.8 %collective-permute-start.3 = (bf16[16,2704]{1,0:T(8,128)(2,1)S(1)}, bf16[16,2704]{1,0:T(8,128)(2,1)S(1)}, u32[]{:S(2)}, u32[]{:S(2)}) collective-permute-start(bf16[16,2704]{1,0:T(8,128)(2,1)S(1)} %pad_maximum_fusion), channel_id=1, source_target_pairs={{0,16},{8,24},{16,0},{24,8},{1,17},{9,25},{17,1},{25,9},{2,18},{10... | collective-permute-start | bytes 259592 | tf_op jit(solution)/shard_map/ppermute | solution.py:80
  8.0 8.7 %collective-permute-start.4 = (bf16[16,2704]{1,0:T(8,128)(2,1)S(1)}, bf16[16,2704]{1,0:T(8,128)(2,1)S(1)}, u32[]{:S(2)}, u32[]{:S(2)}) collective-permute-start(bf16[16,2704]{1,0:T(8,128)(2,1)S(1)} %pad_maximum_fusion), channel_id=1, source_target_pairs={{0,24},{8,16},{16,8},{24,0},{1,25},{9,17},{17,9},{25,1},{2,26},{10... | collective-permute-start | bytes 259592 | tf_op jit(solution)/shard_map/ppermute | solution.py:80
  8.0 10.2 %collective-permute-start.5 = (bf16[16,2704]{1,0:T(8,128)(2,1)S(1)}, bf16[16,2704]{1,0:T(8,128)(2,1)S(1)}, u32[]{:S(2)}, u32[]{:S(2)}) collective-permute-start(bf16[16,2704]{1,0:T(8,128)(2,1)S(1)} %pad_maximum_fusion), channel_id=1, source_target_pairs={{0,2},{2,0},{1,3},{3,1},{4,6},{6,4},{5,7},{7,5},{8,10},{10,8},{9,1... | collective-permute-start | bytes 259592 | tf_op jit(solution)/shard_map/ppermute | solution.py:80
  8.0 16.4 %collective-permute-start = (bf16[48,2704]{1,0:T(8,128)(2,1)}, bf16[48,2704]{1,0:T(8,128)(2,1)S(1)}, u32[]{:S(2)}, u32[]{:S(2)}) collective-permute-start(bf16[48,2704]{1,0:T(8,128)(2,1)} %param.8), channel_id=1, source_target_pairs={{0,4},{4,0},{1,5},{5,1},{2,6},{6,2},{3,7},{7,3},{8,12},{12,8},{9,1... | collective-permute-start | bytes 778760 | tf_op jit(solution)/shard_map/ppermute | solution.py:80
  9.7 8.5 %collective-permute-start.6 = (bf16[16,2704]{1,0:T(8,128)(2,1)S(1)}, bf16[16,2704]{1,0:T(8,128)(2,1)S(1)}, u32[]{:S(2)}, u32[]{:S(2)}) collective-permute-start(bf16[16,2704]{1,0:T(8,128)(2,1)S(1)} %collective-permute-done.2), channel_id=1, source_target_pairs={{0,2},{2,0},{1,3},{3,1},{4,6},{6,4},{5,7},{7,5},{8,10},{10,8},{9,1... | collective-permute-start | bytes 259592 | tf_op jit(solution)/shard_map/ppermute | solution.py:80
  15.2 9.2 %collective-permute-start.1 = (bf16[48,2652]{1,0:T(8,128)(2,1)}, bf16[48,2652]{1,0:T(8,128)(2,1)S(1)}, u32[]{:S(2)}, u32[]{:S(2)}) collective-permute-start(bf16[48,2652]{1,0:T(8,128)(2,1)} %param.9), channel_id=1, source_target_pairs={{0,1},{1,0},{2,3},{3,2},{4,5},{5,4},{6,7},{7,6},{8,9},{9,8},{10,11... | collective-permute-start | bytes 763784 | tf_op jit(solution)/shard_map/ppermute | solution.py:80
  16.8 6.5 %collective-permute-start.11 = (bf16[48,2652]{1,0:T(8,128)(2,1)}, bf16[48,2652]{1,0:T(8,128)(2,1)S(1)}, u32[]{:S(2)}, u32[]{:S(2)}) collective-permute-start(bf16[48,2652]{1,0:T(8,128)(2,1)} %param.9), channel_id=1, source_target_pairs={{0,4},{4,0},{1,5},{5,1},{2,6},{6,2},{3,7},{7,3},{8,12},{12,8},{9,1... | collective-permute-start | bytes 763784 | tf_op jit(solution)/shard_map/ppermute | solution.py:80
  18.2 1.4 %collective-permute-start.7 = (bf16[16,2704]{1,0:T(8,128)(2,1)S(1)}, bf16[16,2704]{1,0:T(8,128)(2,1)S(1)}, u32[]{:S(2)}, u32[]{:S(2)}) collective-permute-start(bf16[16,2704]{1,0:T(8,128)(2,1)S(1)} %collective-permute-done.3), channel_id=1, source_target_pairs={{0,2},{2,0},{1,3},{3,1},{4,6},{6,4},{5,7},{7,5},{8,10},{10,8},{9,1... | collective-permute-start | bytes 259592 | tf_op jit(solution)/shard_map/ppermute | solution.py:80
  18.3 6.1 %collective-permute-start.8 = (bf16[16,2704]{1,0:T(8,128)(2,1)S(1)}, bf16[16,2704]{1,0:T(8,128)(2,1)S(1)}, u32[]{:S(2)}, u32[]{:S(2)}) collective-permute-start(bf16[16,2704]{1,0:T(8,128)(2,1)S(1)} %collective-permute-done.4), channel_id=1, source_target_pairs={{0,2},{2,0},{1,3},{3,1},{4,6},{6,4},{5,7},{7,5},{8,10},{10,8},{9,1... | collective-permute-start | bytes 259592 | tf_op jit(solution)/shard_map/ppermute | solution.py:80
  19.7 9.6 %collective-permute-start.9 = (bf16[48,2704]{1,0:T(8,128)(2,1)}, bf16[48,2704]{1,0:T(8,128)(2,1)S(1)}, u32[]{:S(2)}, u32[]{:S(2)}) collective-permute-start(bf16[48,2704]{1,0:T(8,128)(2,1)} %param.8), channel_id=1, source_target_pairs={{0,1},{1,0},{2,3},{3,2},{4,5},{5,4},{6,7},{7,6},{8,9},{9,8},{10,11... | collective-permute-start | bytes 778760 | tf_op jit(solution)/shard_map/ppermute | solution.py:80
  23.3 10.7 %collective-permute-start.12 = (bf16[48,2652]{1,0:T(8,128)(2,1)S(1)}, bf16[48,2652]{1,0:T(8,128)(2,1)S(1)}, u32[]{:S(2)}, u32[]{:S(2)}) collective-permute-start(bf16[48,2652]{1,0:T(8,128)(2,1)S(1)} %collective-permute-done.11), channel_id=1, source_target_pairs={{0,1},{1,0},{2,3},{3,2},{4,5},{5,4},{6,7},{7,6},{8,9},{9,8},{10,11... | collective-permute-start | bytes 763784 | tf_op jit(solution)/shard_map/ppermute | solution.py:80
  24.5 9.5 %copy-start.2 = (bf16[48,2652]{1,0:T(8,128)(2,1)S(1)}, bf16[48,2652]{1,0:T(8,128)(2,1)}, u32[]{:S(2)}) copy-start(bf16[48,2652]{1,0:T(8,128)(2,1)} %param.9) | copy-start | bytes 763780
  29.4 6.8 %copy-start.1 = (bf16[48,2704]{1,0:T(8,128)(2,1)S(1)}, bf16[48,2704]{1,0:T(8,128)(2,1)}, u32[]{:S(2)}) copy-start(bf16[48,2704]{1,0:T(8,128)(2,1)} %param.8) | copy-start | bytes 778756
  29.4 6.8 %collective-permute-start.10 = (bf16[48,2704]{1,0:T(8,128)(2,1)S(1)}, bf16[48,2704]{1,0:T(8,128)(2,1)S(1)}, u32[]{:S(2)}, u32[]{:S(2)}) collective-permute-start(bf16[48,2704]{1,0:T(8,128)(2,1)S(1)} %collective-permute-done.9), channel_id=1, source_target_pairs={{0,4},{4,0},{1,5},{5,1},{2,6},{6,2},{3,7},{7,3},{8,12},{12,8},{9,1... | collective-permute-start | bytes 778760 | tf_op jit(solution)/shard_map/ppermute | solution.py:80
  37.1 12.2 %copy-start = (bf16[16,2652]{1,0:T(8,128)(2,1)S(1)}, bf16[16,2652]{1,0:T(8,128)(2,1)}, u32[]{:S(2)}) copy-start(bf16[16,2652]{1,0:T(8,128)(2,1)} %param.7) | copy-start | bytes 254596
  37.1 1.7 %collective-permute-start.13 = (bf16[64,2652]{1,0:T(8,128)(2,1)S(1)}, bf16[64,2652]{1,0:T(8,128)(2,1)S(1)}, u32[]{:S(2)}, u32[]{:S(2)}) collective-permute-start(bf16[64,2652]{1,0:T(8,128)(2,1)S(1)} %convolution_convert_fusion), channel_id=1, source_target_pairs={{0,2},{2,0},{1,3},{3,1},{4,6},{6,4},{5,7},{7,5},{8,10},{10,8},{9,1... | collective-permute-start | bytes 1018376 | tf_op jit(solution)/shard_map/ppermute | solution.py:80
  39.2 6.0 %collective-permute-start.14 = (bf16[16,2652]{1,0:T(8,128)(2,1)S(1)}, bf16[16,2652]{1,0:T(8,128)(2,1)S(1)}, u32[]{:S(2)}, u32[]{:S(2)}) collective-permute-start(bf16[16,2652]{1,0:T(8,128)(2,1)S(1)} %get-tuple-element.48), channel_id=1, source_target_pairs={{0,8},{8,0},{16,24},{24,16},{1,9},{9,1},{17,25},{25,17},{2,10},{10... | collective-permute-start | bytes 254600 | tf_op jit(solution)/shard_map/ppermute | solution.py:80
  39.3 10.0 %collective-permute-start.15 = (bf16[16,2652]{1,0:T(8,128)(2,1)S(1)}, bf16[16,2652]{1,0:T(8,128)(2,1)S(1)}, u32[]{:S(2)}, u32[]{:S(2)}) collective-permute-start(bf16[16,2652]{1,0:T(8,128)(2,1)S(1)} %get-tuple-element.50), channel_id=1, source_target_pairs={{0,16},{8,24},{16,0},{24,8},{1,17},{9,25},{17,1},{25,9},{2,18},{10... | collective-permute-start | bytes 254600 | tf_op jit(solution)/shard_map/ppermute | solution.py:80
  42.3 7.0 %collective-permute-start.16 = (bf16[16,2652]{1,0:T(8,128)(2,1)S(1)}, bf16[16,2652]{1,0:T(8,128)(2,1)S(1)}, u32[]{:S(2)}, u32[]{:S(2)}) collective-permute-start(bf16[16,2652]{1,0:T(8,128)(2,1)S(1)} %get-tuple-element.49), channel_id=1, source_target_pairs={{0,24},{8,16},{16,8},{24,0},{1,25},{9,17},{17,9},{25,1},{2,26},{10... | collective-permute-start | bytes 254600 | tf_op jit(solution)/shard_map/ppermute | solution.py:80
  50.1 4.7 %collective-permute-start.17 = (bf16[16,2652]{1,0:T(8,128)(2,1)S(1)}, bf16[16,2652]{1,0:T(8,128)(2,1)S(1)}, u32[]{:S(2)}, u32[]{:S(2)}) collective-permute-start(bf16[16,2652]{1,0:T(8,128)(2,1)S(1)} %get-tuple-element.39), channel_id=1, source_target_pairs={{0,8},{8,0},{16,24},{24,16},{1,9},{9,1},{17,25},{25,17},{2,10},{10... | collective-permute-start | bytes 254600 | tf_op jit(solution)/shard_map/ppermute | solution.py:80
  51.9 9.1 %collective-permute-start.18 = (bf16[16,2652]{1,0:T(8,128)(2,1)S(1)}, bf16[16,2652]{1,0:T(8,128)(2,1)S(1)}, u32[]{:S(2)}, u32[]{:S(2)}) collective-permute-start(bf16[16,2652]{1,0:T(8,128)(2,1)S(1)} %get-tuple-element.39), channel_id=1, source_target_pairs={{0,16},{8,24},{16,0},{24,8},{1,17},{9,25},{17,1},{25,9},{2,18},{10... | collective-permute-start | bytes 254600 | tf_op jit(solution)/shard_map/ppermute | solution.py:80
  53.4 7.6 %collective-permute-start.19 = (bf16[16,2652]{1,0:T(8,128)(2,1)S(1)}, bf16[16,2652]{1,0:T(8,128)(2,1)S(1)}, u32[]{:S(2)}, u32[]{:S(2)}) collective-permute-start(bf16[16,2652]{1,0:T(8,128)(2,1)S(1)} %get-tuple-element.39), channel_id=1, source_target_pairs={{0,24},{8,16},{16,8},{24,0},{1,25},{9,17},{17,9},{25,1},{2,26},{10... | collective-permute-start | bytes 254600 | tf_op jit(solution)/shard_map/ppermute | solution.py:80
  54.6 6.9 %collective-permute-start.20 = (bf16[16,2652]{1,0:T(8,128)(2,1)S(1)}, bf16[16,2652]{1,0:T(8,128)(2,1)S(1)}, u32[]{:S(2)}, u32[]{:S(2)}) collective-permute-start(bf16[16,2652]{1,0:T(8,128)(2,1)S(1)} %get-tuple-element.39), channel_id=1, source_target_pairs={{0,2},{2,0},{1,3},{3,1},{4,6},{6,4},{5,7},{7,5},{8,10},{10,8},{9,1... | collective-permute-start | bytes 254600 | tf_op jit(solution)/shard_map/ppermute | solution.py:80
  54.7 6.9 %collective-permute-start.21 = (bf16[16,2652]{1,0:T(8,128)(2,1)S(1)}, bf16[16,2652]{1,0:T(8,128)(2,1)S(1)}, u32[]{:S(2)}, u32[]{:S(2)}) collective-permute-start(bf16[16,2652]{1,0:T(8,128)(2,1)S(1)} %collective-permute-done.17), channel_id=1, source_target_pairs={{0,2},{2,0},{1,3},{3,1},{4,6},{6,4},{5,7},{7,5},{8,10},{10,8},{9,1... | collective-permute-start | bytes 254600 | tf_op jit(solution)/shard_map/ppermute | solution.py:80
  61.0 1.3 %collective-permute-start.22 = (bf16[16,2652]{1,0:T(8,128)(2,1)S(1)}, bf16[16,2652]{1,0:T(8,128)(2,1)S(1)}, u32[]{:S(2)}, u32[]{:S(2)}) collective-permute-start(bf16[16,2652]{1,0:T(8,128)(2,1)S(1)} %collective-permute-done.18), channel_id=1, source_target_pairs={{0,2},{2,0},{1,3},{3,1},{4,6},{6,4},{5,7},{7,5},{8,10},{10,8},{9,1... | collective-permute-start | bytes 254600 | tf_op jit(solution)/shard_map/ppermute | solution.py:80
  61.0 1.5 %collective-permute-start.23 = (bf16[16,2652]{1,0:T(8,128)(2,1)S(1)}, bf16[16,2652]{1,0:T(8,128)(2,1)S(1)}, u32[]{:S(2)}, u32[]{:S(2)}) collective-permute-start(bf16[16,2652]{1,0:T(8,128)(2,1)S(1)} %collective-permute-done.19), channel_id=1, source_target_pairs={{0,2},{2,0},{1,3},{3,1},{4,6},{6,4},{5,7},{7,5},{8,10},{10,8},{9,1... | collective-permute-start | bytes 254600 | tf_op jit(solution)/shard_map/ppermute | solution.py:80
  64.7 9.2 %collective-permute-start.30 = (bf16[48,2652]{1,0:T(8,128)(2,1)S(1)}, bf16[48,2652]{1,0:T(8,128)(2,1)S(1)}, u32[]{:S(2)}, u32[]{:S(2)}) collective-permute-start(bf16[48,2652]{1,0:T(8,128)(2,1)S(1)} %convolution_convert_fusion.1), channel_id=1, source_target_pairs={{0,1},{1,0},{2,3},{3,2},{4,5},{5,4},{6,7},{7,6},{8,9},{9,8},{10,11... | collective-permute-start | bytes 763784 | tf_op jit(solution)/shard_map/ppermute | solution.py:80
  65.8 16.0 %collective-permute-start.28 = (bf16[48,2652]{1,0:T(8,128)(2,1)S(1)}, bf16[48,2652]{1,0:T(8,128)(2,1)S(1)}, u32[]{:S(2)}, u32[]{:S(2)}) collective-permute-start(bf16[48,2652]{1,0:T(8,128)(2,1)S(1)} %convolution_convert_fusion.2), channel_id=1, source_target_pairs={{0,4},{4,0},{1,5},{5,1},{2,6},{6,2},{3,7},{7,3},{8,12},{12,8},{9,1... | collective-permute-start | bytes 763784 | tf_op jit(solution)/shard_map/ppermute | solution.py:80
  66.9 12.1 %collective-permute-start.26 = (bf16[48,2704]{1,0:T(8,128)(2,1)S(1)}, bf16[48,2704]{1,0:T(8,128)(2,1)S(1)}, u32[]{:S(2)}, u32[]{:S(2)}) collective-permute-start(bf16[48,2704]{1,0:T(8,128)(2,1)S(1)} %convolution_convert_fusion.3), channel_id=1, source_target_pairs={{0,1},{1,0},{2,3},{3,2},{4,5},{5,4},{6,7},{7,6},{8,9},{9,8},{10,11... | collective-permute-start | bytes 778760 | tf_op jit(solution)/shard_map/ppermute | solution.py:80
  67.5 13.2 %collective-permute-start.24 = (bf16[48,2704]{1,0:T(8,128)(2,1)S(1)}, bf16[48,2704]{1,0:T(8,128)(2,1)S(1)}, u32[]{:S(2)}, u32[]{:S(2)}) collective-permute-start(bf16[48,2704]{1,0:T(8,128)(2,1)S(1)} %convolution_convert_fusion.4), channel_id=1, source_target_pairs={{0,4},{4,0},{1,5},{5,1},{2,6},{6,2},{3,7},{7,3},{8,12},{12,8},{9,1... | collective-permute-start | bytes 778760 | tf_op jit(solution)/shard_map/ppermute | solution.py:80
  73.9 9.6 %collective-permute-start.31 = (bf16[24,2652]{1,0:T(8,128)(2,1)S(1)}, bf16[24,2652]{1,0:T(8,128)(2,1)S(1)}, u32[]{:S(2)}, u32[]{:S(2)}) collective-permute-start(bf16[24,2652]{1,0:T(8,128)(2,1)S(1)} %get-tuple-element.44), channel_id=1, source_target_pairs={{0,4},{4,0},{1,5},{5,1},{2,6},{6,2},{3,7},{7,3},{8,12},{12,8},{9,1... | collective-permute-start | bytes 381896 | tf_op jit(solution)/shard_map/ppermute | solution.py:80
  79.1 8.4 %collective-permute-start.27 = (bf16[24,2704]{1,0:T(8,128)(2,1)S(1)}, bf16[24,2704]{1,0:T(8,128)(2,1)S(1)}, u32[]{:S(2)}, u32[]{:S(2)}) collective-permute-start(bf16[24,2704]{1,0:T(8,128)(2,1)S(1)} %get-tuple-element.40), channel_id=1, source_target_pairs={{0,4},{4,0},{1,5},{5,1},{2,6},{6,2},{3,7},{7,3},{8,12},{12,8},{9,1... | collective-permute-start | bytes 389384 | tf_op jit(solution)/shard_map/ppermute | solution.py:80
  80.7 6.7 %collective-permute-start.25 = (bf16[24,2704]{1,0:T(8,128)(2,1)S(1)}, bf16[24,2704]{1,0:T(8,128)(2,1)S(1)}, u32[]{:S(2)}, u32[]{:S(2)}) collective-permute-start(bf16[24,2704]{1,0:T(8,128)(2,1)S(1)} %get-tuple-element.42), channel_id=1, source_target_pairs={{0,1},{1,0},{2,3},{3,2},{4,5},{5,4},{6,7},{7,6},{8,9},{9,8},{10,11... | collective-permute-start | bytes 389384 | tf_op jit(solution)/shard_map/ppermute | solution.py:80
  81.8 5.6 %collective-permute-start.29 = (bf16[24,2652]{1,0:T(8,128)(2,1)S(1)}, bf16[24,2652]{1,0:T(8,128)(2,1)S(1)}, u32[]{:S(2)}, u32[]{:S(2)}) collective-permute-start(bf16[24,2652]{1,0:T(8,128)(2,1)S(1)} %get-tuple-element.46), channel_id=1, source_target_pairs={{0,1},{1,0},{2,3},{3,2},{4,5},{5,4},{6,7},{7,6},{8,9},{9,8},{10,11... | collective-permute-start | bytes 381896 | tf_op jit(solution)/shard_map/ppermute | solution.py:80
  89.1 10.8 %all-to-all-start = ((f32[32,1,128]{2,1,0:T(1,128)}), f32[32,1,128]{2,1,0:T(1,128)S(1)}, u32[]{:S(2)}, u32[]{:S(2)}) async-start(f32[32,1,128]{2,1,0:T(1,128)} %bitcast.4), calls=%async_computation | async-start | bytes 32768 | tf_op jit(solution)/shard_map/all_to_all | solution.py:201
